TPU v7x, 32 devices: a whole 2x2x4 slice. The times are simulated.
32 devices in a mesh: dp: 4 (over x, core), fsdp: 8 (over z, y).
Axes of the slice: x: 2, y: 2, z: 4, core: 2. Of those that a mesh axis runs over, the one named last changes fastest.
Arguments:
- frames: bfloat16 [32768, 1024], P(('dp', 'fsdp')), may hold values from -6 to 6
- clip_lengths: int32 [128], P(('dp', 'fsdp')), may hold values from 0 to 1024, as said below
- timesteps: int32 [128], P(('dp', 'fsdp')), may hold values from 0 to 999
- cotangent: bfloat16 [32768, 1024], P(('dp', 'fsdp')), may hold values from -6 to 6
- adaptive_weight: bfloat16 [1024, 6144], P('fsdp', 'dp'), may hold values from -0.1875 to 0.1875
- project_weight: bfloat16 [1024, 3072], P('fsdp', 'dp'), may hold values from -0.1875 to 0.1875
- output_weight: bfloat16 [1024, 1024], P('fsdp', 'dp'), may hold values from -0.5 to 0.5
- upward_weight: bfloat16 [1024, 2048], P('fsdp', 'dp'), may hold values from -0.1875 to 0.1875
- downward_weight: bfloat16 [2048, 1024], P('fsdp', 'dp'), may hold values from -0.25 to 0.25
Outputs:
- block_out: bfloat16 [32768, 1024], P(('dp', 'fsdp'))
- frames_grad: float32 [32768, 1024], P(('dp', 'fsdp'))
- adaptive_grad: float32 [1024, 6144], P('fsdp', 'dp')
- project_grad: float32 [1024, 3072], P('fsdp', 'dp')
- output_grad: float32 [1024, 1024], P('fsdp', 'dp')
- upward_grad: float32 [1024, 2048], P('fsdp', 'dp')
- downward_grad: float32 [2048, 1024], P('fsdp', 'dp')
Inputs may be any that keep to these rules, and one draw needn't show every extreme that they name: `clip_lengths`: the clips of one device take at most 1024 slots together; in every draw some device holds a single clip of 1024 frames.
All inputs are finite; a program needn't handle non-finite values.
Results may differ from a plain program's by a relative error of at most 0.01.
Values may be sent and summed in bfloat16 or wider, within the bound.
A program may use at most 384 MiB of HBM per device.

v0:
```python
import math

import jax
import jax.numpy as jnp
from jax import lax
from jax.sharding import PartitionSpec as P

HEADS = 16
HEAD_DIM = 64


EPSILON = 1e-06
HIGHEST = lax.Precision.HIGHEST


def layer_norm(values):
    center = values - jnp.mean(values, axis=-1, keepdims=True)
    spread = jnp.mean(center * center, axis=-1, keepdims=True)
    return center * lax.rsqrt(spread + EPSILON)


def gelu_tanh(values):
    return jax.nn.gelu(values, approximate=True)


def clip_layout(lengths, frame_count):
    clip_count = lengths.shape[0]
    endings = jnp.cumsum(lengths, dtype=jnp.int32)
    beginnings = endings - lengths
    frame_index = jnp.arange(frame_count, dtype=jnp.int32)
    segment = jnp.sum(
        (frame_index[:, None] >= endings[None, :]).astype(jnp.int32), axis=1, dtype=jnp.int32
    )
    member = segment[:, None] == jnp.arange(clip_count, dtype=jnp.int32)[None, :]
    position = frame_index - jnp.sum(
        jnp.where(member, beginnings[None, :], 0), axis=1, dtype=jnp.int32
    )
    onehot = member.astype(jnp.float32)
    validity = (segment < clip_count).astype(jnp.float32)[:, None]
    return (segment, onehot, validity, position)


def time_table(steps, model_width):
    halfway = model_width // 2
    rates = jnp.exp(-math.log(10000.0) * jnp.arange(halfway, dtype=jnp.float32) / (halfway - 1))
    angles = steps.astype(jnp.float32)[:, None] * rates[None, :]
    return jnp.concatenate([jnp.sin(angles), jnp.cos(angles)], axis=-1)


def rotary_table(position, head_width):
    halfway = head_width // 2
    rates = jnp.exp(-math.log(10000.0) * jnp.arange(halfway, dtype=jnp.float32) / halfway)
    angles = position.astype(jnp.float32)[:, None] * rates[None, :]
    cosine = jnp.cos(angles)
    sine_table = jnp.sin(angles)
    return (
        jnp.concatenate([cosine, cosine], axis=-1),
        jnp.concatenate([sine_table, sine_table], axis=-1),
    )


def rotate(values, cosine, sine_table):
    halfway = values.shape[-1] // 2
    turned = jnp.concatenate([-values[..., halfway:], values[..., :halfway]], axis=-1)
    return values * cosine[:, None, :] + turned * sine_table[:, None, :]


def rotate_back(values, cosine, sine_table):
    halfway = values.shape[-1] // 2
    scaled = values * sine_table[:, None, :]
    turned = jnp.concatenate([scaled[..., halfway:], -scaled[..., :halfway]], axis=-1)
    return values * cosine[:, None, :] + turned


def attend_forward(queries, keys_low, values_low, segment):
    frame_count = queries.shape[0]
    block_rows = min(512, frame_count)
    scale = queries.shape[-1] ** (-0.5)
    outputs = []
    log_parts = []
    for row_start in range(0, frame_count, block_rows):
        query_block = queries[row_start : row_start + block_rows]
        scores = (
            jnp.einsum("qhd,khd->hqk", query_block, keys_low, preferred_element_type=jnp.float32)
            * scale
        )
        allowed = segment[row_start : row_start + block_rows, None] == segment[None, :]
        scores = jnp.where(allowed[None], scores, -1000000000.0)
        maximum = jnp.max(scores, axis=-1, keepdims=True)
        exponent = jnp.exp(scores - maximum)
        row_total = jnp.sum(exponent, axis=-1, keepdims=True)
        weights_low = (exponent / row_total).astype(jnp.bfloat16)
        outputs.append(
            jnp.einsum("hqk,khd->qhd", weights_low, values_low, preferred_element_type=jnp.float32)
        )
        log_parts.append(maximum + jnp.log(row_total))
    return (jnp.concatenate(outputs, axis=0), jnp.concatenate(log_parts, axis=1))


def attend_backward(queries, keys_low, values_low, segment, log_totals, grad_mixed):
    frame_count = queries.shape[0]
    block_rows = min(512, frame_count)
    scale = queries.shape[-1] ** (-0.5)
    grad_keys = jnp.zeros(keys_low.shape, jnp.float32)
    grad_values = jnp.zeros(values_low.shape, jnp.float32)
    query_parts = []
    for row_start in range(0, frame_count, block_rows):
        query_block = queries[row_start : row_start + block_rows]
        grad_block = grad_mixed[row_start : row_start + block_rows]
        scores = (
            jnp.einsum("qhd,khd->hqk", query_block, keys_low, preferred_element_type=jnp.float32)
            * scale
        )
        allowed = segment[row_start : row_start + block_rows, None] == segment[None, :]
        scores = jnp.where(allowed[None], scores, -1000000000.0)
        probs = jnp.exp(scores - log_totals[:, row_start : row_start + block_rows])
        grad_values = grad_values + jnp.einsum(
            "hqk,qhd->khd",
            probs.astype(jnp.bfloat16),
            grad_block,
            preferred_element_type=jnp.float32,
        )
        grad_probs = jnp.einsum(
            "qhd,khd->hqk", grad_block, values_low, preferred_element_type=jnp.float32
        )
        inner = jnp.sum(grad_probs * probs, axis=-1, keepdims=True)
        grad_scores = (probs * (grad_probs - inner)).astype(jnp.bfloat16)
        query_parts.append(
            jnp.einsum("hqk,khd->qhd", grad_scores, keys_low, preferred_element_type=jnp.float32)
            * scale
        )
        grad_keys = (
            grad_keys
            + jnp.einsum(
                "hqk,qhd->khd", grad_scores, query_block, preferred_element_type=jnp.float32
            )
            * scale
        )
    return (jnp.concatenate(query_parts, axis=0), grad_keys, grad_values)


def per_device(
    frames,
    clip_lengths,
    timesteps,
    cotangent,
    adaptive_weight,
    project_weight,
    output_weight,
    upward_weight,
    downward_weight,
):
    frame_count = frames.shape[0]
    model_width = frames.shape[1]
    head_shape = (frame_count, HEADS, HEAD_DIM)
    segment, onehot, validity, position = clip_layout(clip_lengths, frame_count)
    cosine, sine_table = rotary_table(position, HEAD_DIM)
    context = jax.nn.silu(time_table(timesteps, model_width)).astype(jnp.bfloat16)
    col_adapt, col_project, col_output, col_upward, col_downward = (
        lax.all_gather(adaptive_weight, "dp", axis=1, tiled=True),
        lax.all_gather(project_weight, "dp", axis=1, tiled=True),
        lax.all_gather(output_weight, "dp", axis=1, tiled=True),
        lax.all_gather(upward_weight, "dp", axis=1, tiled=True),
        lax.all_gather(downward_weight, "dp", axis=1, tiled=True),
    )
    full_adapt, full_project, full_output, full_upward, full_downward = (
        lax.all_gather(col_adapt, "fsdp", axis=0, tiled=True),
        lax.all_gather(col_project, "fsdp", axis=0, tiled=True),
        lax.all_gather(col_output, "fsdp", axis=0, tiled=True),
        lax.all_gather(col_upward, "fsdp", axis=0, tiled=True),
        lax.all_gather(col_downward, "fsdp", axis=0, tiled=True),
    )
    inputs_f = frames.astype(jnp.float32)
    modulation = jnp.dot(context, full_adapt, preferred_element_type=jnp.float32)
    per_frame = jnp.dot(onehot, modulation, precision=HIGHEST, preferred_element_type=jnp.float32)
    shift_one, scale_one, gate_one, shift_two, scale_two, gate_two = jnp.split(per_frame, 6, axis=1)
    normed_one, norm_back_one = jax.vjp(layer_norm, inputs_f)
    attn_in = (normed_one * (1.0 + scale_one) + shift_one).astype(jnp.bfloat16)
    projected = jnp.dot(attn_in, full_project, preferred_element_type=jnp.float32)
    queries = rotate(projected[:, :model_width].reshape(head_shape), cosine, sine_table).astype(
        jnp.bfloat16
    )
    keys_low = rotate(
        projected[:, model_width : 2 * model_width].reshape(head_shape), cosine, sine_table
    ).astype(jnp.bfloat16)
    values_low = projected[:, 2 * model_width :].reshape(head_shape).astype(jnp.bfloat16)
    mixed, log_totals = attend_forward(queries, keys_low, values_low, segment)
    attn_out = mixed.reshape(frame_count, model_width).astype(jnp.bfloat16)
    branch = jnp.dot(attn_out, full_output, preferred_element_type=jnp.float32)
    middle = inputs_f + validity * gate_one * branch
    normed_two, norm_back_two = jax.vjp(layer_norm, middle)
    ffn_in = (normed_two * (1.0 + scale_two) + shift_two).astype(jnp.bfloat16)
    upward_act = jnp.dot(ffn_in, full_upward, preferred_element_type=jnp.float32)
    hidden_f, gelu_back = jax.vjp(gelu_tanh, upward_act)
    hidden = hidden_f.astype(jnp.bfloat16)
    downward_act = jnp.dot(hidden, full_downward, preferred_element_type=jnp.float32)
    block_out = (middle + validity * gate_two * downward_act).astype(jnp.bfloat16)
    again_project, again_output, again_upward, again_downward = (
        lax.all_gather(project_weight, "dp", axis=1, tiled=True),
        lax.all_gather(output_weight, "dp", axis=1, tiled=True),
        lax.all_gather(upward_weight, "dp", axis=1, tiled=True),
        lax.all_gather(downward_weight, "dp", axis=1, tiled=True),
    )
    back_project, back_output, back_upward, back_downward = (
        lax.all_gather(again_project, "fsdp", axis=0, tiled=True),
        lax.all_gather(again_output, "fsdp", axis=0, tiled=True),
        lax.all_gather(again_upward, "fsdp", axis=0, tiled=True),
        lax.all_gather(again_downward, "fsdp", axis=0, tiled=True),
    )
    grad_out = cotangent.astype(jnp.float32)
    grad_down = (validity * gate_two * grad_out).astype(jnp.bfloat16)
    grad_gate_two = validity * downward_act * grad_out
    downward_local = jnp.einsum("fi,fo->io", hidden, grad_down, preferred_element_type=jnp.float32)
    grad_hidden = jnp.einsum(
        "fo,io->fi", grad_down, back_downward, preferred_element_type=jnp.float32
    )
    grad_up = gelu_back(grad_hidden)[0].astype(jnp.bfloat16)
    upward_local = jnp.einsum("fi,fo->io", ffn_in, grad_up, preferred_element_type=jnp.float32)
    grad_ffn_in = jnp.einsum("fo,io->fi", grad_up, back_upward, preferred_element_type=jnp.float32)
    grad_middle = grad_out + norm_back_two(grad_ffn_in * (1.0 + scale_two))[0]
    grad_branch = (validity * gate_one * grad_middle).astype(jnp.bfloat16)
    grad_gate_one = validity * branch * grad_middle
    output_local = jnp.einsum(
        "fi,fo->io", attn_out, grad_branch, preferred_element_type=jnp.float32
    )
    grad_mixed = (
        jnp.einsum("fo,io->fi", grad_branch, back_output, preferred_element_type=jnp.float32)
        .astype(jnp.bfloat16)
        .reshape(head_shape)
    )
    grad_queries, grad_keys, grad_values = attend_backward(
        queries, keys_low, values_low, segment, log_totals, grad_mixed
    )
    grad_projected = jnp.concatenate(
        [
            rotate_back(grad_queries, cosine, sine_table).reshape(frame_count, model_width),
            rotate_back(grad_keys, cosine, sine_table).reshape(frame_count, model_width),
            grad_values.reshape(frame_count, model_width),
        ],
        axis=1,
    ).astype(jnp.bfloat16)
    project_local = jnp.einsum(
        "fi,fo->io", attn_in, grad_projected, preferred_element_type=jnp.float32
    )
    grad_attn_in = jnp.einsum(
        "fo,io->fi", grad_projected, back_project, preferred_element_type=jnp.float32
    )
    frames_grad = grad_middle + norm_back_one(grad_attn_in * (1.0 + scale_one))[0]
    grad_per_frame = jnp.concatenate(
        [
            grad_attn_in,
            grad_attn_in * normed_one,
            grad_gate_one,
            grad_ffn_in,
            grad_ffn_in * normed_two,
            grad_gate_two,
        ],
        axis=1,
    )
    grad_modulation = jnp.einsum(
        "fc,fm->cm", onehot, grad_per_frame, precision=HIGHEST, preferred_element_type=jnp.float32
    ).astype(jnp.bfloat16)
    adaptive_local = jnp.einsum(
        "cd,cm->dm", context, grad_modulation, preferred_element_type=jnp.float32
    )
    rows_adapt, rows_project, rows_output, rows_upward, rows_downward = (
        lax.psum_scatter(adaptive_local, "fsdp", scatter_dimension=0, tiled=True),
        lax.psum_scatter(project_local, "fsdp", scatter_dimension=0, tiled=True),
        lax.psum_scatter(output_local, "fsdp", scatter_dimension=0, tiled=True),
        lax.psum_scatter(upward_local, "fsdp", scatter_dimension=0, tiled=True),
        lax.psum_scatter(downward_local, "fsdp", scatter_dimension=0, tiled=True),
    )
    adaptive_grad, project_grad, output_grad, upward_grad, downward_grad = (
        lax.psum_scatter(rows_adapt, "dp", scatter_dimension=1, tiled=True),
        lax.psum_scatter(rows_project, "dp", scatter_dimension=1, tiled=True),
        lax.psum_scatter(rows_output, "dp", scatter_dimension=1, tiled=True),
        lax.psum_scatter(rows_upward, "dp", scatter_dimension=1, tiled=True),
        lax.psum_scatter(rows_downward, "dp", scatter_dimension=1, tiled=True),
    )
    return (
        block_out,
        frames_grad,
        adaptive_grad,
        project_grad,
        output_grad,
        upward_grad,
        downward_grad,
    )


def solution(mesh):
    return jax.shard_map(
        per_device,
        mesh=mesh,
        in_specs=(
            P(("dp", "fsdp"), None),
            P(("dp", "fsdp")),
            P(("dp", "fsdp")),
            P(("dp", "fsdp"), None),
            P("fsdp", "dp"),
            P("fsdp", "dp"),
            P("fsdp", "dp"),
            P("fsdp", "dp"),
            P("fsdp", "dp"),
        ),
        out_specs=(
            P(("dp", "fsdp"), None),
            P(("dp", "fsdp"), None),
            P("fsdp", "dp"),
            P("fsdp", "dp"),
            P("fsdp", "dp"),
            P("fsdp", "dp"),
            P("fsdp", "dp"),
        ),
        check_vma=False,
    )
```

profile of v0, /device:TPU:0, one launch (start us, length us, event | category | flops | bytes accessed | tf_op | source)
XLA Modules:
  0.0 1716.6 jit_solution(714754443547720409)
XLA Ops:
  8.0 24.0 %all-gather.7.cloned.1.call-done = bf16[128,6144]{1,0:T(8,128)(2,1)} async-done(((bf16[128,1536]{1,0:T(8,128)(2,1)}), bf16[128,6144]{1,0:T(8,128)(2,1)}) %all-gather.7.cloned.1.call-update) | async-done | bytes 1572880 | tf_op jit(solution)/shard_map/all_gather | solution.py:160
  70.2 140.1 %all-gather.9.cloned.1.call-done = bf16[1024,6144]{1,0:T(8,128)(2,1)} async-done(((bf16[128,6144]{1,0:T(8,128)(2,1)}), bf16[1024,6144]{1,0:T(8,128)(2,1)}) %all-gather.9.cloned.1.call-update) | async-done | bytes 12582928 | tf_op jit(solution)/shard_map/all_gather | solution.py:167
  216.6 19.3 %fusion.55 = f32[1024,6144]{1,0:T(8,128)S(1)} fusion(f32[4,6144]{1,0:T(4,128)S(1)} %fusion.65, s32[1024]{0:T(1024)S(1)} %convert_reduce_fusion.1), kind=kOutput, calls=%fused_computation.121 | convolution fusion | flops 301993984 | bytes 25268224 | tf_op jit(solution)/shard_map/dot_general | solution.py:175
  246.6 62.8 %all-gather.11.cloned.1.call-done = bf16[1024,3072]{1,0:T(8,128)(2,1)} async-done(((bf16[128,3072]{1,0:T(8,128)(2,1)}), bf16[1024,3072]{1,0:T(8,128)(2,1)}) %all-gather.11.cloned.1.call-update) | async-done | bytes 6291472 | tf_op jit(solution)/shard_map/all_gather | solution.py:168
  350.1 13.8 fusion.77
  363.9 14.1 fusion.78
  378.0 14.3 fusion.1
  392.3 13.3 fusion.49
  405.6 14.4 fusion
  420.0 12.8 fusion.48
  463.2 42.2 %all-gather.15.cloned.1.call-done = bf16[1024,2048]{1,0:T(8,128)(2,1)} async-done(((bf16[128,2048]{1,0:T(8,128)(2,1)}), bf16[1024,2048]{1,0:T(8,128)(2,1)}) %all-gather.15.cloned.1.call-update) | async-done | bytes 4194320 | tf_op jit(solution)/shard_map/all_gather | solution.py:170
  505.4 14.3 fusion.18
  528.1 16.4 fusion.70
  571.0 13.1 fusion.67
  585.7 22.7 %multiply_reduce_fusion.1 = (f32[16,512]{1,0:T(8,128)S(1)}, f32[16,512,1024]{2,1,0:T(8,128)}) fusion(f32[16,512,1024]{2,1,0:T(8,128)} %get-tuple-element.48, f32[16,512]{1,0:T(8,128)S(1)} %log_add_fusion.1, bf16[512,16,64]{0,2,1:T(8,128)(2,1)S(1)} %bitcast.86, bf16[1024,16,64]{0,2,1:T(8,128)(2,1)S(1)} %bitcast.81), kind=kOutput, calls=%fused_computation.4 | convolution fusion | flops 1098899456 | bytes 70320128 | tf_op jit(solution)/shard_map/qhd,khd->hqk/dot_general | solution.py:123
  608.4 28.5 %multiply_convert_fusion.1 = bf16[16,512,1024]{2,1,0:T(8,128)(2,1)} fusion(f32[16,512,1024]{2,1,0:T(8,128)} %get-tuple-element.56, f32[16,512,1024]{2,1,0:T(8,128)} %get-tuple-element.48, f32[16,512]{1,0:T(8,128)S(1)} %get-tuple-element.55, f32[16,512]{1,0:T(8,128)S(1)} %log_add_fusion.1), kind=kLoop, calls=%fused_computation.3 | loop fusion | flops 33554432 | bytes 83951616 | tf_op jit(solution)/shard_map/convert_element_type | solution.py:127
  636.9 12.5 convolution_multiply_fusion.1
  649.4 24.0 %multiply_reduce_fusion = (f32[16,512]{1,0:T(8,128)S(1)}, f32[16,512,1024]{2,1,0:T(8,128)}) fusion(f32[16,512,1024]{2,1,0:T(8,128)} %get-tuple-element.46, f32[16,512]{1,0:T(8,128)S(1)} %log_add_fusion, bf16[512,16,64]{0,2,1:T(8,128)(2,1)S(1)} %bitcast.88, bf16[1024,16,64]{0,2,1:T(8,128)(2,1)} %bitcast.80), kind=kOutput, calls=%fused_computation.1 | convolution fusion | flops 1098899456 | bytes 70320128 | tf_op jit(solution)/shard_map/qhd,khd->hqk/dot_general | solution.py:123
  673.5 28.8 %multiply_convert_fusion = bf16[16,512,1024]{2,1,0:T(8,128)(2,1)} fusion(f32[16,512,1024]{2,1,0:T(8,128)} %get-tuple-element.58, f32[16,512,1024]{2,1,0:T(8,128)} %get-tuple-element.46, f32[16,512]{1,0:T(8,128)S(1)} %get-tuple-element.57, f32[16,512]{1,0:T(8,128)S(1)} %log_add_fusion), kind=kLoop, calls=%fused_computation | loop fusion | flops 33554432 | bytes 83951616 | tf_op jit(solution)/shard_map/convert_element_type | solution.py:127
  702.3 12.6 convolution_multiply_fusion
  750.2 16.2 fusion.4
  766.4 15.2 add_convert_fusion
  781.6 15.0 fusion.42
  833.2 12.4 convolution_convert_fusion
  857.4 85.0 %reduce-scatter.27.cloned.1.call-done = f32[256,1024]{1,0:T(8,128)} async-done(((f32[2048,1024]{1,0:T(8,128)}), f32[256,1024]{1,0:T(8,128)}) %reduce-scatter.27.cloned.1.call-update) | async-done | bytes 1048592 | tf_op jit(solution)/shard_map/reduce_scatter | solution.py:271
  942.5 209.9 %reduce-scatter.15.cloned.1.call-done = f32[128,3072]{1,0:T(8,128)} async-done(((f32[1024,3072]{1,0:T(8,128)}), f32[128,3072]{1,0:T(8,128)}) %reduce-scatter.15.cloned.1.call-update) | async-done | bytes 1572880 | tf_op jit(solution)/shard_map/reduce_scatter | solution.py:268
  1152.5 406.2 %reduce-scatter.11.cloned.1.call-done = f32[128,6144]{1,0:T(8,128)} async-done(((f32[1024,6144]{1,0:T(8,128)}), f32[128,6144]{1,0:T(8,128)}) %reduce-scatter.11.cloned.1.call-update) | async-done | bytes 3145744 | tf_op jit(solution)/shard_map/reduce_scatter | solution.py:267
  1558.7 23.7 %reduce-scatter.21.cloned.1.call-done = f32[128,256]{1,0:T(8,128)} async-done(((f32[128,1024]{1,0:T(8,128)}), f32[128,256]{1,0:T(8,128)}) %reduce-scatter.21.cloned.1.call-update) | async-done | bytes 131088 | tf_op jit(solution)/shard_map/reduce_scatter | solution.py:276
  1582.4 27.9 %reduce-scatter.25.cloned.1.call-done = f32[128,512]{1,0:T(8,128)} async-done(((f32[128,2048]{1,0:T(8,128)}), f32[128,512]{1,0:T(8,128)}) %reduce-scatter.25.cloned.1.call-update) | async-done | bytes 262160 | tf_op jit(solution)/shard_map/reduce_scatter | solution.py:277
  1610.3 27.8 %reduce-scatter.29.cloned.1.call-done = f32[256,256]{1,0:T(8,128)} async-done(((f32[256,1024]{1,0:T(8,128)}), f32[256,256]{1,0:T(8,128)}) %reduce-scatter.29.cloned.1.call-update) | async-done | bytes 262160 | tf_op jit(solution)/shard_map/reduce_scatter | solution.py:278
  1638.1 31.0 %reduce-scatter.17.cloned.1.call-done = f32[128,768]{1,0:T(8,128)} async-done(((f32[128,3072]{1,0:T(8,128)}), f32[128,768]{1,0:T(8,128)}) %reduce-scatter.17.cloned.1.call-update) | async-done | bytes 393232 | tf_op jit(solution)/shard_map/reduce_scatter | solution.py:275
  1669.1 40.8 %reduce-scatter.13.cloned.1.call-done = f32[128,1536]{1,0:T(8,128)} async-done(((f32[128,6144]{1,0:T(8,128)}), f32[128,1536]{1,0:T(8,128)}) %reduce-scatter.13.cloned.1.call-update) | async-done | bytes 786448 | tf_op jit(solution)/shard_map/reduce_scatter | solution.py:274
  (252 shorter events, 246.6 us)
Async XLA Ops:
  7.2 42.5 %copy-start.44 = (bf16[256,256]{1,0:T(8,128)(2,1)S(1)}, bf16[256,256]{1,0:T(8,128)(2,1)}, u32[]{:S(2)}) copy-start(bf16[256,256]{1,0:T(8,128)(2,1)} %param.17) | copy-start | bytes 393220
  7.2 50.3 %copy-start.45 = (bf16[128,512]{1,0:T(8,128)(2,1)S(1)}, bf16[128,512]{1,0:T(8,128)(2,1)}, u32[]{:S(2)}) copy-start(bf16[128,512]{1,0:T(8,128)(2,1)} %param.16) | copy-start | bytes 393220
  7.2 58.1 %copy-start.67 = (s32[4]{0:T(128)S(1)}, s32[4]{0:T(128)}, u32[]{:S(2)}) copy-start(s32[4]{0:T(128)} %param.10) | copy-start | bytes 52
  7.2 59.0 %copy-start.68 = (s32[4]{0:T(128)S(1)}, s32[4]{0:T(128)}, u32[]{:S(2)}) copy-start(s32[4]{0:T(128)} %param.11) | copy-start | bytes 52
  7.2 59.1 %copy-start.3 = (bf16[1024,1024]{1,0:T(8,128)(2,1)S(1)}, bf16[1024,1024]{1,0:T(8,128)(2,1)}, u32[]{:S(2)}) copy-start(bf16[1024,1024]{1,0:T(8,128)(2,1)} %param.9) | copy-start | bytes 6291460
  7.2 24.8 %all-gather.7.cloned.1.call-start = ((), (), s32[]{:S(2)}) async-start(), calls=%async_computation.10 | async-start | bytes 1966080 | tf_op jit(solution)/shard_map/all_gather | solution.py:160
  8.0 202.4 %all-gather.9.cloned.1.call-start = ((), (), s32[]{:S(2)}) async-start(), calls=%async_computation.11 | async-start | bytes 14155776 | tf_op jit(solution)/shard_map/all_gather | solution.py:167
  32.0 277.4 %all-gather.11.cloned.1.call-start = ((), (), s32[]{:S(2)}) async-start(), calls=%async_computation.12 | async-start | bytes 7077888 | tf_op jit(solution)/shard_map/all_gather | solution.py:168
  41.5 392.9 %all-gather.13.cloned.1.call-start = ((), (), s32[]{:S(2)}) async-start(), calls=%async_computation.13 | async-start | bytes 2359296 | tf_op jit(solution)/shard_map/all_gather | solution.py:169
  49.6 402.9 %all-gather.17.cloned.1.call-start = ((), (), s32[]{:S(2)}) async-start(), calls=%async_computation.15 | async-start | bytes 4718592 | tf_op jit(solution)/shard_map/all_gather | solution.py:171
  57.4 448.0 %all-gather.15.cloned.1.call-start = ((), (), s32[]{:S(2)}) async-start(), calls=%async_computation.14 | async-start | bytes 4718592 | tf_op jit(solution)/shard_map/all_gather | solution.py:170
  65.2 790.9 %reduce-scatter.19.cloned.1.call-start = ((), (), s32[]{:S(2)}) async-start(), calls=%async_computation.20 | async-start | bytes 4718592 | tf_op jit(solution)/shard_map/reduce_scatter | solution.py:269
  65.6 151.1 %copy-start.40 = (s32[1024]{0:T(1024)}, s32[1024]{0:T(1024)S(1)}, u32[]{:S(2)}) copy-start(s32[1024]{0:T(1024)S(1)} %convert_reduce_fusion.1) | copy-start | bytes 12292
  66.6 169.3 %copy-start.50 = (f32[1024]{0:T(1024)}, f32[1024]{0:T(1024)S(1)}, u32[]{:S(2)}) copy-start(f32[1024]{0:T(1024)S(1)} %broadcast_multiply_fusion.3) | copy-start | bytes 12292
  67.9 168.1 %copy-start.58 = (f32[1024]{0:T(1024)}, f32[1024]{0:T(1024)S(1)}, u32[]{:S(2)}) copy-start(f32[1024]{0:T(1024)S(1)} %fusion.59) | copy-start | bytes 12292
  68.1 148.5 %copy-start.52 = (f32[4,512]{1,0:T(4,128)}, f32[4,512]{1,0:T(4,128)S(1)}, u32[]{:S(2)}) copy-start(f32[4,512]{1,0:T(4,128)S(1)} %get-tuple-element.43) | copy-start | bytes 24580
  68.1 148.5 %copy-start.54 = (f32[4,512]{1,0:T(4,128)}, f32[4,512]{1,0:T(4,128)S(1)}, u32[]{:S(2)}) copy-start(f32[4,512]{1,0:T(4,128)S(1)} %get-tuple-element.44) | copy-start | bytes 24580
  69.6 276.6 %copy-start.31 = (f32[1024,64]{0,1:T(8,128)}, f32[1024,64]{0,1:T(8,128)S(1)}, u32[]{:S(2)}) copy-start(f32[1024,64]{0,1:T(8,128)S(1)} %get-tuple-element.36) | copy-start | bytes 786436
  332.9 87.1 %copy-start.13 = (bf16[1024,1024]{0,1:T(8,128)(2,1)}, bf16[1024,1024]{0,1:T(8,128)(2,1)S(1)}, u32[]{:S(2)}) copy-start(bf16[1024,1024]{0,1:T(8,128)(2,1)S(1)} %copy.49) | copy-start | bytes 6291460
  446.0 82.0 %copy-start.56 = (f32[1024]{0:T(1024)}, f32[1024]{0:T(1024)S(1)}, u32[]{:S(2)}) copy-start(f32[1024]{0:T(1024)S(1)} %broadcast_multiply_fusion.2) | copy-start | bytes 12292
  448.0 80.1 %copy-start.60 = (f32[1024]{0:T(1024)}, f32[1024]{0:T(1024)S(1)}, u32[]{:S(2)}) copy-start(f32[1024]{0:T(1024)S(1)} %fusion.60) | copy-start | bytes 12292
  554.5 302.2 %reduce-scatter.23.cloned.1.call-start = ((), (), s32[]{:S(2)}) async-start(), calls=%async_computation.22 | async-start | bytes 9437184 | tf_op jit(solution)/shard_map/reduce_scatter | solution.py:270
  563.5 379.0 %reduce-scatter.27.cloned.1.call-start = ((), (), s32[]{:S(2)}) async-start(), calls=%async_computation.24 | async-start | bytes 9437184 | tf_op jit(solution)/shard_map/reduce_scatter | solution.py:271
  584.1 568.3 %reduce-scatter.15.cloned.1.call-start = ((), (), s32[]{:S(2)}) async-start(), calls=%async_computation.18 | async-start | bytes 14155776 | tf_op jit(solution)/shard_map/reduce_scatter | solution.py:268
  608.4 28.5 %copy-start.47 = (f32[16,512]{1,0:T(8,128)S(1)}, f32[16,512]{1,0:T(8,128)}, u32[]{:S(2)}) copy-start(f32[16,512]{1,0:T(8,128)} %copy-done.46) | copy-start | bytes 98308
  608.4 28.5 %copy-start.2 = (bf16[1024,16,64]{0,2,1:T(8,128)(2,1)S(1)}, bf16[1024,16,64]{0,2,1:T(8,128)(2,1)}, u32[]{:S(2)}) copy-start(bf16[1024,16,64]{0,2,1:T(8,128)(2,1)} %copy-done.1) | copy-start | bytes 6291460
  796.6 762.1 %reduce-scatter.11.cloned.1.call-start = ((), (), s32[]{:S(2)}) async-start(), calls=%async_computation.16 | async-start | bytes 28311552 | tf_op jit(solution)/shard_map/reduce_scatter | solution.py:267
  856.0 726.4 %reduce-scatter.21.cloned.1.call-start = ((), (), s32[]{:S(2)}) async-start(), calls=%async_computation.21 | async-start | bytes 655360 | tf_op jit(solution)/shard_map/reduce_scatter | solution.py:276
  856.6 753.7 %reduce-scatter.25.cloned.1.call-start = ((), (), s32[]{:S(2)}) async-start(), calls=%async_computation.23 | async-start | bytes 1310720 | tf_op jit(solution)/shard_map/reduce_scatter | solution.py:277
  857.4 780.8 %reduce-scatter.29.cloned.1.call-start = ((), (), s32[]{:S(2)}) async-start(), calls=%async_computation.25 | async-start | bytes 1310720 | tf_op jit(solution)/shard_map/reduce_scatter | solution.py:278
  942.5 726.7 %reduce-scatter.17.cloned.1.call-start = ((), (), s32[]{:S(2)}) async-start(), calls=%async_computation.19 | async-start | bytes 1966080 | tf_op jit(solution)/shard_map/reduce_scatter | solution.py:275
  1152.5 557.4 %reduce-scatter.13.cloned.1.call-start = ((), (), s32[]{:S(2)}) async-start(), calls=%async_computation.17 | async-start | bytes 3932160 | tf_op jit(solution)/shard_map/reduce_scatter | solution.py:274
  (58 other events, 485.5 us)
Sparse Core Ops, SparseCore 0:
  9.6 22.3 all-gather.6
  34.2 176.0 all-gather.8
  212.5 96.8 all-gather.10
  311.4 47.2 all-gather.12
  360.7 71.3 all-gather.16
  434.0 71.3 all-gather.14
  554.6 86.8 reduce-scatter.18
  645.1 147.0 reduce-scatter.22
  795.9 146.5 reduce-scatter.26
  945.9 206.5 reduce-scatter.14
  1156.3 402.3 reduce-scatter.10
  1561.6 20.7 reduce-scatter.20
  1585.5 24.7 reduce-scatter.24
  1613.3 24.7 reduce-scatter.28
  1641.1 28.0 reduce-scatter.16
  1672.1 37.7 reduce-scatter.12
where the time goes:
time: 1730 us; the launch traced here: 1720 us
  waiting for transfers between devices  1120 us (65%)
  matrix products  354 us (20%)
  other arithmetic  144 us (8%)
  local copies, waits for them, and re-layouts  45.8 us (3%)
  blocking collectives  32.9 us (2%)
    reduce_scatter x1, waiting for transfers between devices, per_device(): lax.psum_scatter(adaptive_local, 'fsdp', scatter_dimension=0, tiled=True)  406 us
    reduce_scatter x1, waiting for transfers between devices, per_device(): lax.psum_scatter(project_local, 'fsdp', scatter_dimension=0, tiled=True)  210 us
    all_gather x1, waiting for transfers between devices, per_device(): lax.all_gather(col_adapt, 'fsdp', axis=0, tiled=True)  140 us
    reduce_scatter x1, waiting for transfers between devices, per_device(): lax.psum_scatter(downward_local, 'fsdp', scatter_dimension=0, tiled=True)  85 us
    all_gather x1, waiting for transfers between devices, per_device(): lax.all_gather(col_project, 'fsdp', axis=0, tiled=True)  62.8 us
    convert_element_type x2, other arithmetic, attend_backward(): grad_scores = (probs * (grad_probs - inner)).astype(jnp.bfloat16)  57.3 us
    dot_general x2, matrix products, attend_backward(): jnp.einsum('qhd,khd->hqk', grad_block, values_low, preferred_element_type...  46.7 us
    all_gather x1, waiting for transfers between devices, per_device(): lax.all_gather(col_upward, 'fsdp', axis=0, tiled=True)  42.2 us
  transfers between devices with their start and end apart: 16, of which 12 were waited for; matrix products, arithmetic and copies ran while one was open for 28% of the time, Pallas kernels for 0%

commit v1 on v0

v1 whole, which is shorter than its diff:
```python
import functools
import math

import jax
import jax.numpy as jnp
from jax import lax
from jax.experimental import pallas as pl
from jax.experimental.pallas import tpu as pltpu
from jax.sharding import PartitionSpec as P

HEAD_DIM = 64
LANES = 128
EPSILON = 1e-06
MASKED = -1000000000.0
VMEM_LIMIT = 60 * 1024 * 1024
BF16 = jnp.bfloat16
F32 = jnp.float32
AXES = ("dp", "fsdp")


def dot_nn(a, b):
    return lax.dot_general(a, b, (((1,), (0,)), ((), ())), preferred_element_type=F32)


def dot_nt(a, b):
    return lax.dot_general(a, b, (((1,), (1,)), ((), ())), preferred_element_type=F32)


def clip_rows(seg, mod_ref, part, width, clips):
    rows = jnp.zeros((seg.shape[0], width), F32)
    for c in range(clips):
        rows = jnp.where(seg == c, mod_ref[c : c + 1, part * width : (part + 1) * width], rows)
    return rows


def norm_parts(values):
    center = values - jnp.mean(values, axis=-1, keepdims=True)
    spread = jnp.mean(center * center, axis=-1, keepdims=True)
    scale = lax.rsqrt(spread + EPSILON)
    return center * scale, scale


def norm_back(grad, normed, scale):
    mean_g = jnp.mean(grad, axis=-1, keepdims=True)
    mean_gn = jnp.mean(grad * normed, axis=-1, keepdims=True)
    return (grad - mean_g - normed * mean_gn) * scale


def clip_sums(member, values):
    high = values.astype(BF16)
    low = (values - high.astype(F32)).astype(BF16)
    return dot_nn(member, high) + dot_nn(member, low)


def turn(values):
    lane = lax.broadcasted_iota(jnp.int32, values.shape, 1) % HEAD_DIM
    half = HEAD_DIM // 2
    return jnp.where(
        lane < half, pltpu.roll(values, LANES - half, 1), pltpu.roll(values, half, 1)
    )


def project_kernel(clips, frames_ref, seg_ref, mod_ref, weight_ref, cos_ref, sin_ref, attn_ref, out_ref):
    width = frames_ref.shape[1]

    @pl.when(pl.program_id(0) == 0)
    def _():
        step = 256
        for r in range(0, frames_ref.shape[0], step):
            normed, _ = norm_parts(frames_ref[r : r + step].astype(F32))
            seg = seg_ref[r : r + step]
            shift = clip_rows(seg, mod_ref, 0, width, clips)
            scale = clip_rows(seg, mod_ref, 1, width, clips)
            attn_ref[r : r + step] = (normed * (1.0 + scale) + shift).astype(BF16)

    result = dot_nn(attn_ref[...], weight_ref[0])
    for c in range(0, result.shape[1], LANES):
        piece = result[:, c : c + LANES]
        out_ref[:, c : c + LANES] = (piece * cos_ref[0] + turn(piece) * sin_ref[0]).astype(BF16)


def project_call(frames, seg_col, mod, weight, cosine, sine, clips):
    count, width = frames.shape
    blocks, _, columns = weight.shape
    tile = 256 if columns % 256 == 0 else 128
    per_block = columns // tile
    per_part = width // tile
    whole = lambda u: (0, 0)
    return pl.pallas_call(
        functools.partial(project_kernel, clips),
        grid=(blocks * per_block,),
        in_specs=[
            pl.BlockSpec((count, width), whole),
            pl.BlockSpec((count, 1), whole),
            pl.BlockSpec(mod.shape, whole),
            pl.BlockSpec((1, width, tile), lambda u: (u // per_block, 0, u % per_block)),
            pl.BlockSpec((1, count, LANES), lambda u: (u // per_part, 0, 0)),
            pl.BlockSpec((1, count, LANES), lambda u: (u // per_part, 0, 0)),
        ],
        out_specs=[
            pl.BlockSpec((count, width), whole),
            pl.BlockSpec((count, tile), lambda u: (0, u)),
        ],
        out_shape=[
            jax.ShapeDtypeStruct((count, width), BF16),
            jax.ShapeDtypeStruct((count, blocks * columns), BF16),
        ],
        compiler_params=pltpu.CompilerParams(vmem_limit_bytes=VMEM_LIMIT),
        cost_estimate=pl.CostEstimate(
            flops=2 * count * width * blocks * columns,
            bytes_accessed=2 * (2 * count * width + width * blocks * columns + count * blocks * columns),
            transcendentals=0,
        ),
        name="project",
    )(frames, seg_col, mod, weight, cosine, sine)


CHUNK = 256


def lane_head(values, h):
    lane = lax.broadcasted_iota(jnp.int32, (1, LANES), 1)
    keep = ((lane >= h * HEAD_DIM) & (lane < (h + 1) * HEAD_DIM)).astype(BF16)
    return values * keep


def transposed(values):
    return values.astype(F32).T.astype(BF16)


def attend_kernel(single_ref, q_ref, k_ref, v_ref, segr_ref, segc_ref, out_ref, lse_ref, mixed):
    keys = k_ref[...]
    values_t = transposed(v_ref[...])
    count = keys.shape[0]

    def run(masked):
        for h in range(LANES // HEAD_DIM):
            rows = slice(h * HEAD_DIM, (h + 1) * HEAD_DIM)
            for start in range(0, count, CHUNK):
                part = slice(start, start + CHUNK)
                scores = dot_nt(keys, lane_head(q_ref[part, :], h))
                if masked:
                    scores = jnp.where(segc_ref[...] == segr_ref[:, part], scores, MASKED)
                top = jnp.max(scores, axis=0, keepdims=True)
                weight = jnp.exp(scores - top)
                total = jnp.sum(weight, axis=0, keepdims=True)
                product = dot_nn(values_t[rows], weight.astype(BF16))
                mixed[rows, part] = product / total
                lse_ref[0, h : h + 1, part] = top + jnp.log(total)

    pl.when(single_ref[0] == 1)(functools.partial(run, False))
    pl.when(single_ref[0] != 1)(functools.partial(run, True))
    out_ref[...] = mixed[...].T.astype(BF16)


def attend_call(single, qkv, seg_row, seg_col):
    count = qkv.shape[0]
    width = qkv.shape[1] // 3
    pairs = width // LANES
    block = lambda t: pl.BlockSpec((count, LANES), lambda p, s: (0, t * pairs + p))
    return pl.pallas_call(
        attend_kernel,
        grid_spec=pltpu.PrefetchScalarGridSpec(
            num_scalar_prefetch=1,
            grid=(pairs,),
            in_specs=[
                block(0),
                block(1),
                block(2),
                pl.BlockSpec((1, count), lambda p, s: (0, 0)),
                pl.BlockSpec((count, 1), lambda p, s: (0, 0)),
            ],
            out_specs=[
                block(0),
                pl.BlockSpec((1, LANES // HEAD_DIM, count), lambda p, s: (p, 0, 0)),
            ],
            scratch_shapes=[pltpu.VMEM((LANES, count), F32)],
        ),
        out_shape=[
            jax.ShapeDtypeStruct((count, width), BF16),
            jax.ShapeDtypeStruct((pairs, LANES // HEAD_DIM, count), F32),
        ],
        compiler_params=pltpu.CompilerParams(vmem_limit_bytes=VMEM_LIMIT),
        cost_estimate=pl.CostEstimate(
            flops=16 * count * count * width, bytes_accessed=8 * count * width, transcendentals=16 * count * count
        ),
        name="attend",
    )(single, qkv, qkv, qkv, seg_row, seg_col)


def attend_back_kernel(
    single_ref, q_ref, k_ref, v_ref, grad_ref, out_ref, lse_ref, segr_ref, segc_ref, cos_ref, sin_ref,
    result_ref, grad_q, grad_k, grad_v,
):
    keys = k_ref[...]
    values = v_ref[...]
    keys_t = transposed(keys)
    count = keys.shape[0]
    inner_t = (grad_ref[...].astype(F32) * out_ref[...].astype(F32)).T
    heads = LANES // HEAD_DIM

    def run(masked):
        for h in range(heads):
            rows = slice(h * HEAD_DIM, (h + 1) * HEAD_DIM)
            inner = jnp.sum(inner_t[rows], axis=0, keepdims=True)
            for start in range(0, count, CHUNK):
                part = slice(start, start + CHUNK)
                query = lane_head(q_ref[part, :], h)
                grad = lane_head(grad_ref[part, :], h)
                scores = dot_nt(keys, query)
                if masked:
                    scores = jnp.where(segc_ref[...] == segr_ref[:, part], scores, MASKED)
                probs = jnp.exp(scores - lse_ref[0, h : h + 1, part])
                grad_probs = dot_nt(values, grad)
                add_v = dot_nn(probs.astype(BF16), grad)
                grad_scores = (probs * (grad_probs - inner[:, part])).astype(BF16)
                add_k = dot_nn(grad_scores, query)
                if h == 0 and start == 0:
                    grad_v[...] = add_v
                    grad_k[...] = add_k
                else:
                    grad_v[...] += add_v
                    grad_k[...] += add_k
                grad_q[rows, part] = dot_nn(keys_t[rows], grad_scores)

    pl.when(single_ref[0] == 1)(functools.partial(run, False))
    pl.when(single_ref[0] != 1)(functools.partial(run, True))

    def back(grad):
        return grad * cos_ref[...] + turn(grad * sin_ref[...])

    result_ref[0] = back(grad_q[...].T * (HEAD_DIM ** -0.5)).astype(BF16)
    result_ref[1] = back(grad_k[...]).astype(BF16)
    result_ref[2] = grad_v[...].astype(BF16)


def attend_back_call(single, qkv, grad_mixed, attn_out, lse, seg_row, seg_col, cosine, sine):
    count, width = attn_out.shape
    pairs = width // LANES
    heads = LANES // HEAD_DIM
    block = lambda t: pl.BlockSpec((count, LANES), lambda p, s: (0, t * pairs + p))
    fixed = lambda shape: pl.BlockSpec(shape, lambda p, s: (0, 0))
    return pl.pallas_call(
        attend_back_kernel,
        grid_spec=pltpu.PrefetchScalarGridSpec(
            num_scalar_prefetch=1,
            grid=(pairs,),
            in_specs=[
                block(0),
                block(1),
                block(2),
                block(0),
                block(0),
                pl.BlockSpec((1, heads, count), lambda p, s: (p, 0, 0)),
                fixed((1, count)),
                fixed((count, 1)),
                fixed((count, LANES)),
                fixed((count, LANES)),
            ],
            out_specs=pl.BlockSpec((3, count, LANES), lambda p, s: (0, 0, p)),
            scratch_shapes=[
                pltpu.VMEM((LANES, count), F32),
                pltpu.VMEM((count, LANES), F32),
                pltpu.VMEM((count, LANES), F32),
            ],
        ),
        out_shape=jax.ShapeDtypeStruct((3, count, width), BF16),
        compiler_params=pltpu.CompilerParams(vmem_limit_bytes=VMEM_LIMIT),
        cost_estimate=pl.CostEstimate(
            flops=40 * count * count * width, bytes_accessed=16 * count * width, transcendentals=16 * count * count
        ),
        name="attend_back",
    )(single, qkv, qkv, qkv, grad_mixed, attn_out, lse, seg_row, seg_col, cosine, sine)


def by_columns(left, weight_ref):
    return jnp.concatenate([dot_nn(left, weight_ref[b]) for b in range(weight_ref.shape[0])], axis=1)


def by_rows(left, weight_ref):
    columns = weight_ref.shape[2]
    total = None
    for b in range(weight_ref.shape[0]):
        term = dot_nt(left[:, b * columns : (b + 1) * columns], weight_ref[b])
        total = term if total is None else total + term
    return total


def middle_kernel(
    clips, frames_ref, cot_ref, attn_ref, seg_ref, member_ref, mod_ref, wo_ref, wu_ref, wd_ref,
    block_ref, ffn_ref, hidden_ref, down_ref, up_ref, gmid_ref, gbranch_ref, gmixed_ref, sums_ref,
):
    width = frames_ref.shape[1]
    seg = seg_ref[...]
    member = member_ref[...]
    cot = cot_ref[...].astype(F32)
    branch = by_columns(attn_ref[...], wo_ref)
    gate_one = clip_rows(seg, mod_ref, 2, width, clips)
    middle = frames_ref[...].astype(F32) + gate_one * branch
    normed, scale_n = norm_parts(middle)
    scale_two = 1.0 + clip_rows(seg, mod_ref, 4, width, clips)
    ffn_in = (normed * scale_two + clip_rows(seg, mod_ref, 3, width, clips)).astype(BF16)
    ffn_ref[...] = ffn_in
    upward = by_columns(ffn_in, wu_ref)
    root = math.sqrt(2.0 / math.pi)
    square = upward * upward
    wave = jnp.tanh(root * upward * (1.0 + 0.044715 * square))
    half = 0.5 * (1.0 + wave)
    hidden = (upward * half).astype(BF16)
    hidden_ref[...] = hidden
    slope = half + 0.5 * upward * (1.0 - wave * wave) * (root * (1.0 + 3.0 * 0.044715 * square))
    downward = by_columns(hidden, wd_ref)
    gate_two = clip_rows(seg, mod_ref, 5, width, clips)
    block_ref[...] = (middle + gate_two * downward).astype(BF16)
    grad_down = (gate_two * cot).astype(BF16)
    down_ref[...] = grad_down
    grad_up = (by_rows(grad_down, wd_ref) * slope).astype(BF16)
    up_ref[...] = grad_up
    grad_ffn = by_rows(grad_up, wu_ref)
    grad_middle = cot + norm_back(grad_ffn * scale_two, normed, scale_n)
    gmid_ref[...] = grad_middle
    grad_branch = (gate_one * grad_middle).astype(BF16)
    gbranch_ref[...] = grad_branch
    gmixed_ref[...] = by_rows(grad_branch, wo_ref).astype(BF16)

    @pl.when(pl.program_id(0) == 0)
    def _():
        sums_ref[...] = jnp.zeros_like(sums_ref)

    for i, values in enumerate(
        (branch * grad_middle, grad_ffn, grad_ffn * normed, downward * cot)
    ):
        sums_ref[:, i * width : (i + 1) * width] += clip_sums(member, values)


def middle_call(frames, cotangent, attn_out, seg_col, member, mod, wo, wu, wd, clips):
    count, width = frames.shape
    hidden = wd.shape[1]
    tile = 256
    rows = lambda w: pl.BlockSpec((tile, w), lambda i: (i, 0))
    fixed2 = lambda a: pl.BlockSpec(a.shape, lambda i: (0, 0))
    held = lambda a: pl.BlockSpec(a.shape, lambda i: (0, 0, 0), pipeline_mode=pl.Buffered(1))
    shape = lambda w, t: jax.ShapeDtypeStruct((count, w), t)
    return pl.pallas_call(
        functools.partial(middle_kernel, clips),
        grid=(count // tile,),
        in_specs=[
            rows(width),
            rows(width),
            rows(width),
            rows(1),
            pl.BlockSpec((member.shape[0], tile), lambda i: (0, i)),
            fixed2(mod),
            held(wo),
            held(wu),
            held(wd),
        ],
        out_specs=[
            rows(width),
            rows(width),
            rows(hidden),
            rows(width),
            rows(hidden),
            rows(width),
            rows(width),
            rows(width),
            pl.BlockSpec((member.shape[0], 4 * width), lambda i: (0, 0)),
        ],
        out_shape=[
            shape(width, BF16),
            shape(width, BF16),
            shape(hidden, BF16),
            shape(width, BF16),
            shape(hidden, BF16),
            shape(width, F32),
            shape(width, BF16),
            shape(width, BF16),
            jax.ShapeDtypeStruct((member.shape[0], 4 * width), F32),
        ],
        compiler_params=pltpu.CompilerParams(vmem_limit_bytes=VMEM_LIMIT),
        cost_estimate=pl.CostEstimate(
            flops=4 * count * width * (width + 2 * hidden),
            bytes_accessed=2 * width * (width + 2 * hidden) + 30 * count * width,
            transcendentals=count * hidden,
        ),
        name="middle",
    )(frames, cotangent, attn_out, seg_col, member, mod, wo, wu, wd)


def tail_kernel(clips, frames_ref, gmid_ref, gp_ref, seg_ref, member_ref, mod_ref, wp_ref, out_ref, sums_ref):
    width = frames_ref.shape[1]
    columns = wp_ref.shape[2]
    step = min(columns, 256) if columns % 256 == 0 else LANES
    grad = None
    for b in range(wp_ref.shape[0]):
        for c in range(0, columns, step):
            at = b * columns + c
            part, col = at // width, at % width
            term = dot_nt(gp_ref[part, :, col : col + step], wp_ref[b, :, c : c + step])
            grad = term if grad is None else grad + term
    normed, scale_n = norm_parts(frames_ref[...].astype(F32))
    scale_one = 1.0 + clip_rows(seg_ref[...], mod_ref, 1, width, clips)
    out_ref[...] = gmid_ref[...] + norm_back(grad * scale_one, normed, scale_n)

    @pl.when(pl.program_id(0) == 0)
    def _():
        sums_ref[...] = jnp.zeros_like(sums_ref)

    member = member_ref[...]
    for i, values in enumerate((grad, grad * normed)):
        sums_ref[:, i * width : (i + 1) * width] += clip_sums(member, values)


def tail_call(frames, grad_middle, grad_projected, seg_col, member, mod, wp, clips):
    count, width = frames.shape
    tile = 256
    rows = lambda w: pl.BlockSpec((tile, w), lambda i: (i, 0))
    return pl.pallas_call(
        functools.partial(tail_kernel, clips),
        grid=(count // tile,),
        in_specs=[
            rows(width),
            rows(width),
            pl.BlockSpec((3, tile, width), lambda i: (0, i, 0)),
            rows(1),
            pl.BlockSpec((member.shape[0], tile), lambda i: (0, i)),
            pl.BlockSpec(mod.shape, lambda i: (0, 0)),
            pl.BlockSpec(wp.shape, lambda i: (0, 0, 0), pipeline_mode=pl.Buffered(1)),
        ],
        out_specs=[rows(width), pl.BlockSpec((member.shape[0], 2 * width), lambda i: (0, 0))],
        out_shape=[
            jax.ShapeDtypeStruct((count, width), F32),
            jax.ShapeDtypeStruct((member.shape[0], 2 * width), F32),
        ],
        compiler_params=pltpu.CompilerParams(vmem_limit_bytes=VMEM_LIMIT),
        cost_estimate=pl.CostEstimate(
            flops=6 * count * width * width, bytes_accessed=6 * width * width + 16 * count * width, transcendentals=0
        ),
        name="tail",
    )(frames, grad_middle, grad_projected, seg_col, member, mod, wp)


def clip_layout(lengths, frame_count):
    clip_count = lengths.shape[0]
    endings = jnp.cumsum(lengths, dtype=jnp.int32)
    beginnings = endings - lengths
    frame_index = jnp.arange(frame_count, dtype=jnp.int32)
    segment = jnp.sum(
        (frame_index[:, None] >= endings[None, :]).astype(jnp.int32), axis=1, dtype=jnp.int32
    )
    member = segment[:, None] == jnp.arange(clip_count, dtype=jnp.int32)[None, :]
    position = frame_index - jnp.sum(
        jnp.where(member, beginnings[None, :], 0), axis=1, dtype=jnp.int32
    )
    return segment, position


def rotary_tables(position):
    half = HEAD_DIM // 2
    rates = jnp.exp(-math.log(10000.0) * jnp.arange(half, dtype=F32) / half)
    angles = position.astype(F32)[:, None] * rates[None, :]
    cosine, sine = jnp.cos(angles), jnp.sin(angles)
    copies = LANES // HEAD_DIM
    return (
        jnp.concatenate([cosine, cosine] * copies, axis=1),
        jnp.concatenate([-sine, sine] * copies, axis=1),
    )


def gather_blocks(weight, blocks):
    full = lax.all_gather(weight, AXES, axis=0, tiled=True)
    return full.reshape(blocks, full.shape[0] // blocks, full.shape[1])


def scatter_blocks(left, right, blocks):
    local = lax.dot_general(left, right, (((0,), (0,)), ((), ())), preferred_element_type=F32).astype(BF16)
    rows = local.shape[0]
    local = local.reshape(rows, blocks, -1).transpose(1, 0, 2).reshape(blocks * rows, -1)
    return lax.psum_scatter(local, AXES, scatter_dimension=0, tiled=True).astype(F32)


def per_device(
    blocks, row_parts, frames, clip_lengths, timesteps, cotangent,
    adaptive_weight, project_weight, output_weight, upward_weight, downward_weight,
):
    count, width = frames.shape
    clips = clip_lengths.shape[0]
    devices = blocks * row_parts
    segment, position = clip_layout(clip_lengths, count)
    seg_row, seg_col = segment[None, :], segment[:, None]
    single = (segment[0] == segment[count - 1]).astype(jnp.int32)[None]
    pad = -clips % 8
    member = (jnp.arange(clips + pad, dtype=jnp.int32)[:, None] == seg_row) & (seg_row < clips)
    member = member.astype(BF16)
    cosine, sine = rotary_tables(position)

    wp = gather_blocks(project_weight, blocks)
    steps = lax.all_to_all(
        jnp.broadcast_to(timesteps[None, :], (devices, clips)), AXES, 0, 0, tiled=True
    ).reshape(-1)
    rows, columns = adaptive_weight.shape
    half = width // 2
    index = lax.axis_index("fsdp") * rows + jnp.arange(rows, dtype=jnp.int32)
    rates = jnp.exp(-math.log(10000.0) * (index % half).astype(F32) / (half - 1))
    angles = steps.astype(F32)[:, None] * rates[None, :]
    table = jnp.where(index[None, :] < half, jnp.sin(angles), jnp.cos(angles))
    context = jax.nn.silu(table).astype(BF16)
    partial_mod = jnp.dot(context, adaptive_weight, preferred_element_type=F32)
    pieces = lax.all_to_all(partial_mod.reshape(devices, clips, columns), AXES, 0, 0, tiled=True)
    mod = jnp.sum(pieces.reshape(blocks, row_parts, clips, columns), axis=1)
    mod = mod.transpose(1, 0, 2).reshape(clips, blocks * columns)
    mod = jnp.pad(mod, ((0, pad), (0, 0)))

    wo = gather_blocks(output_weight, blocks)
    wu = gather_blocks(upward_weight, blocks)
    wd = gather_blocks(downward_weight, blocks)

    scale = HEAD_DIM ** -0.5
    one = jnp.ones_like(cosine)
    attn_in, qkv = project_call(
        frames, seg_col, mod, wp,
        jnp.stack([cosine * scale, cosine, one]),
        jnp.stack([sine * scale, sine, 0.0 * one]),
        clips,
    )
    attn_out, lse = attend_call(single, qkv, seg_row, seg_col)
    block_out, ffn_in, hidden, grad_down, grad_up, grad_middle, grad_branch, grad_mixed, sums_two = middle_call(
        frames, cotangent, attn_out, seg_col, member, mod, wo, wu, wd, clips
    )
    downward_grad = scatter_blocks(hidden, grad_down, blocks)
    upward_grad = scatter_blocks(ffn_in, grad_up, blocks)
    output_grad = scatter_blocks(attn_out, grad_branch, blocks)
    grad_projected = attend_back_call(
        single, qkv, grad_mixed, attn_out, lse, seg_row, seg_col, cosine, sine
    )
    flat = grad_projected.transpose(1, 0, 2).reshape(count, 3 * width)
    project_grad = scatter_blocks(attn_in, flat, blocks)
    frames_grad, sums_one = tail_call(
        frames, grad_middle, grad_projected, seg_col, member, mod, wp, clips
    )
    grad_mod = jnp.concatenate([sums_one, sums_two], axis=1)[:clips].astype(BF16)
    grad_mod = grad_mod.reshape(clips, blocks, columns).transpose(1, 0, 2)
    grad_mod = jnp.broadcast_to(grad_mod[:, None], (blocks, row_parts, clips, columns))
    grad_all = lax.all_to_all(grad_mod.reshape(devices, clips, columns), AXES, 0, 0, tiled=True)
    adaptive_grad = lax.dot_general(
        context, grad_all.reshape(devices * clips, columns), (((0,), (0,)), ((), ())), preferred_element_type=F32
    )
    return (block_out, frames_grad, adaptive_grad, project_grad, output_grad, upward_grad, downward_grad)


def solution(mesh):
    data = P(AXES, None)
    flat = P(AXES)
    weight = P("fsdp", "dp")
    return jax.shard_map(
        functools.partial(per_device, mesh.shape["dp"], mesh.shape["fsdp"]),
        mesh=mesh,
        in_specs=(data, flat, flat, data) + (weight,) * 5,
        out_specs=(data, data) + (weight,) * 5,
        check_vma=False,
    )
```

time: 1730 us -> 886 us (0.51)
  waiting for transfers between devices: 1120 us -> 537 us
  matrix products: 354 us -> 35.2 us
  Pallas kernels: 0 us -> 182 us
  other arithmetic: 144 us -> 18.2 us
    reduce_scatter x10 -> x4, waiting for transfers between devices: 852 us -> 370 us  [scatter_blocks(): lax.psum_scatter(local, AXES, scatter_dimension=0, tiled=True).astype(F32)]
    dot_general x28 -> x6, matrix products: 354 us -> 35.2 us  [the longest x4 33.1 us: scatter_blocks(): lax.dot_general(left, right, (((0,), (0,)), ((), ())), preferred_element_...]
    pallas_call x0 -> x5, Pallas kernels: none -> 182 us  [the longest x1 55.1 us: attend_back_call(): pl.pallas_call(attend_back_kernel, grid_spec=pltpu.PrefetchScalarGridSpec...]
    all_gather x6 -> x4, waiting for transfers between devices: 269 us -> 139 us  [gather_blocks(): full = lax.all_gather(weight, AXES, axis=0, tiled=True)]
    convert_element_type x9 -> x7, other arithmetic: 72.7 us -> 7.13 us  [the longest x4 6.46 us: scatter_blocks(): lax.psum_scatter(local, AXES, scatter_dimension=0, tiled=True).astype(F32)]
    reduce_sum x6 -> x1, other arithmetic: 33.9 us -> 0.09 us  [per_device(): mod = jnp.sum(pieces.reshape(blocks, row_parts, clips, columns), axis=1)]
    all_gather x4 -> x0, blocking collectives: 32.9 us -> none  [the longest x1 9.47 us: per_device(): lax.all_gather(project_weight, 'dp', axis=1, tiled=True)]
    transpose x0 -> x6, local copies, waits for them, and re-layouts: none -> 28.9 us  [the longest x4 20.1 us: scatter_blocks(): local.reshape(rows, blocks, -1).transpose(1, 0, 2)]
  transfers between devices with their start and end apart: 16 -> 10, of which waited for: 12 -> 8; matrix products, arithmetic and copies ran while one was open for 28% -> 11% of each run, Pallas kernels for 0% -> 16%
where the time goes in v1:
time: 886 us; the launch traced here: 876 us
  waiting for transfers between devices  537 us (61%)
  Pallas kernels  182 us (21%)
  local copies, waits for them, and re-layouts  57.4 us (6%)
  matrix products  35.2 us (4%)
  blocking collectives  19.9 us (2%)
  other arithmetic  18.2 us (2%)
  between operations  16.1 us (2%)
  starting transfers between devices  11.2 us (1%)
    reduce_scatter x4, waiting for transfers between devices, scatter_blocks(): lax.psum_scatter(local, AXES, scatter_dimension=0, tiled=True).astype(F32)  370 us
    all_gather x4, waiting for transfers between devices, gather_blocks(): full = lax.all_gather(weight, AXES, axis=0, tiled=True)  139 us
    pallas_call x1, Pallas kernels, attend_back_call(): pl.pallas_call(attend_back_kernel, grid_spec=pltpu.PrefetchScalarGridSpec...  55.1 us
    pallas_call x1, Pallas kernels, attend_call(): pl.pallas_call(attend_kernel, grid_spec=pltpu.PrefetchScalarGridSpec(num_...  50.7 us
    pallas_call x1, Pallas kernels, middle_call(): pl.pallas_call(functools.partial(middle_kernel, clips), grid=(count // ti...  38.9 us
    dot_general x4, matrix products, scatter_blocks(): lax.dot_general(left, right, (((0,), (0,)), ((), ())), preferred_element_...  33.1 us
    all_to_all x1, waiting for transfers between devices, per_device(): lax.all_to_all(partial_mod.reshape(devices, clips, columns), AXES, 0, 0,...  22.6 us
    pallas_call x1, Pallas kernels, project_call(): pl.pallas_call(functools.partial(project_kernel, clips), grid=(blocks * p...  21.1 us
  transfers between devices with their start and end apart: 10, of which 8 were waited for; matrix products, arithmetic and copies ran while one was open for 11% of the time, Pallas kernels for 16%

profile of v1, /device:TPU:0, one launch (start us, length us, event | category | flops | bytes accessed | tf_op | source)
XLA Modules:
  0.0 876.3 jit_solution(9772757842153421294)
XLA Ops:
  11.2 7.3 all-to-all-start
  23.4 2.3 all-to-all-done
  27.5 3.6 all-to-all-start.1
  31.1 1.9 fusion.2
  39.0 22.6 %all-to-all-done.1 = f32[32,4,1536]{2,1,0:T(4,128)S(1)} async-done(((f32[32,4,1536]{2,1,0:T(4,128)}), f32[32,4,1536]{2,1,0:T(4,128)S(1)}, u32[]{:S(2)}, u32[]{:S(2)}) %all-to-all-start.1) | async-done | bytes 786464 | tf_op jit(solution)/shard_map/all_to_all | solution.py:509
  62.4 25.6 %all-gather.5.cloned.1.call-done = bf16[4096,768]{1,0:T(8,128)(2,1)} async-done(((bf16[128,768]{1,0:T(8,128)(2,1)}), bf16[4096,768]{1,0:T(8,128)(2,1)}) %all-gather.5.cloned.1.call-update) | async-done | bytes 6291472 | tf_op jit(solution)/shard_map/all_gather | solution.py:471
  87.9 21.1 %project.1 = (bf16[1024,1024]{1,0:T(8,128)(2,1)}, bf16[1024,3072]{1,0:T(8,128)(2,1)}) custom-call(bf16[1024,1024]{1,0:T(8,128)(2,1)} %frames_ref.5, s32[1024,1]{1,0:T(8,128)} %copy.43.seg_ref.segc_ref, f32[8,6144]{1,0:T(8,128)} %pad.4.mod_ref, bf16[4,1024,768]{2,1,0:T(8,128)(2,1)} %bitcast.69, f32[3,1024,128]{2,1,0:T(8,128)} %maximum_maximum_fusion.cos_ref, ...), custom_call_target="tpu_custom_call" | custom-call | flops 6442450944 | bytes 16777216 | tf_op jit(solution)/shard_map/project/pallas_call | solution.py:89
  109.1 50.7 %attend.1 = (bf16[1024,1024]{1,0:T(8,128)(2,1)}, f32[8,2,1024]{2,1,0:T(2,128)}) custom-call(s32[1]{0:T(128)S(6)} %convert_element_type.65.single_ref, bf16[1024,3072]{1,0:T(8,128)(2,1)} %get-tuple-element.22.q_ref.k_ref.v_ref, bf16[1024,3072]{1,0:T(8,128)(2,1)} %get-tuple-element.22.q_ref.k_ref.v_ref, ...), custom_call_target="tpu_custom_call" | custom-call | flops 17179869184 | bytes 8388608 | tf_op jit(solution)/shard_map/attend/pallas_call | solution.py:161
  159.8 49.8 %all-gather.9.cloned.1.call-done = bf16[4096,512]{1,0:T(8,128)(2,1)} async-done(((bf16[128,512]{1,0:T(8,128)(2,1)}), bf16[4096,512]{1,0:T(8,128)(2,1)}) %all-gather.9.cloned.1.call-update) | async-done | bytes 4194320 | tf_op jit(solution)/shard_map/all_gather | solution.py:471
  209.5 63.5 %all-gather.11.cloned.1.call-done = bf16[8192,256]{1,0:T(8,128)(2,1)} async-done(((bf16[256,256]{1,0:T(8,128)(2,1)}), bf16[8192,256]{1,0:T(8,128)(2,1)}) %all-gather.11.cloned.1.call-update) | async-done | bytes 4194320 | tf_op jit(solution)/shard_map/all_gather | solution.py:471
  273.0 38.9 %middle.1 = (bf16[1024,1024]{1,0:T(8,128)(2,1)}, bf16[1024,1024]{1,0:T(8,128)(2,1)}, bf16[1024,2048]{1,0:T(8,128)(2,1)}, bf16[1024,1024]{1,0:T(8,128)(2,1)}, bf1...) custom-call(bf16[1024,1024]{1,0:T(8,128)(2,1)} %frames_ref.5, ...), custom_call_target="tpu_custom_call" | custom-call | flops 21474836480 | bytes 41943040 | tf_op jit(solution)/shard_map/middle/pallas_call | solution.py:344
  311.9 4.6 convolution_convert_fusion.3
  316.5 2.6 copy.51
  320.7 8.5 convolution_convert_fusion.2
  329.2 7.9 reshape.439
  337.1 5.0 copy.52
  342.2 1.5 copy-done.12
  343.7 8.3 convolution_convert_fusion.1
  352.0 6.3 copy.53
  359.6 55.1 %attend_back.1.gp_ref = bf16[3,1024,1024]{2,1,0:T(8,128)(2,1)} custom-call(s32[1]{0:T(128)S(6)} %convert_element_type.65.single_ref, bf16[1024,3072]{1,0:T(8,128)(2,1)} %get-tuple-element.22.q_ref.k_ref.v_ref, bf16[1024,3072]{1,0:T(8,128)(2,1)} %get-tuple-element.22.q_ref.k_ref.v_ref, bf16[1024,3072]{1,0:T(8,128)(2,1)} %get-tuple-element.22.q_ref.k_ref.v_ref, ...), custom_call_target="tpu_custom_call" | custom-call | flops 42949672960 | bytes 16777216 | tf_op jit(solution)/shard_map/attend_back/pallas_call | solution.py:243
  414.7 8.8 %copy.49 = bf16[1024,3,1024]{0,2,1:T(8,128)(2,1)} copy(bf16[1024,3,1024]{2,0,1:T(8,128)(2,1)} %bitcast.58) | data formatting | bytes 12582912 | tf_op jit(solution)/shard_map/transpose | solution.py:536
  423.5 11.7 %convolution_convert_fusion = bf16[1024,3072]{1,0:T(8,128)(2,1)} fusion(bf16[1024,1024]{1,0:T(8,128)(2,1)S(1)} %copy-done.11, bf16[1024,3072]{0,1:T(8,128)(2,1)} %bitcast.59), kind=kOutput, calls=%fused_computation | convolution fusion | flops 6445596672 | bytes 14680064 | tf_op jit(solution)/shard_map/dot_general | solution.py:476
  435.2 12.3 %reshape.435 = bf16[1024,4,768]{2,1,0:T(4,128)(2,1)} reshape(bf16[1024,3072]{1,0:T(8,128)(2,1)} %convolution_convert_fusion) | data formatting | bytes 12582912 | tf_op jit(solution)/shard_map/reshape | solution.py:478
  447.6 6.2 copy.50
  453.8 15.8 %tail.1 = (f32[1024,1024]{1,0:T(8,128)}, f32[8,2048]{1,0:T(8,128)}) custom-call(bf16[1024,1024]{1,0:T(8,128)(2,1)} %frames_ref.5, f32[1024,1024]{1,0:T(8,128)} %get-tuple-element.25.gmid_ref, bf16[3,1024,1024]{2,1,0:T(8,128)(2,1)} %attend_back.1.gp_ref, s32[1024,1]{1,0:T(8,128)} %copy.43.seg_ref.segc_ref, bf16[8,1024]{1,0:T(8,128)(2,1)} %fusion.12.member_ref, ...), custom_call_target="tpu_custom_call" | custom-call | flops 6442450944 | bytes 23068672 | tf_op jit(solution)/shard_map/tail/pallas_call | solution.py:418
  470.7 19.9 %all_to_all.16 = bf16[32,4,1536]{2,1,0:T(4,128)(2,1)S(1)} all-to-all(bf16[32,4,1536]{2,1,0:T(4,128)(2,1)S(1)} %bitcast.62), channel_id=1, replica_groups=mesh['dp'=4,'fsdp'=8] {'dp','fsdp'}, dimensions={0} | all-to-all | bytes 786432 | tf_op jit(solution)/shard_map/all_to_all | solution.py:544
  493.7 109.6 %reduce-scatter.9.cloned.1.call-done = bf16[128,512]{1,0:T(8,128)(2,1)} async-done(((bf16[4096,512]{1,0:T(8,128)(2,1)}), bf16[128,512]{1,0:T(8,128)(2,1)}) %reduce-scatter.9.cloned.1.call-update) | async-done | bytes 131088 | tf_op jit(solution)/shard_map/reduce_scatter | solution.py:479
  603.3 1.6 convert_element_type.77
  604.9 144.5 %reduce-scatter.11.cloned.1.call-done = bf16[256,256]{1,0:T(8,128)(2,1)} async-done(((bf16[8192,256]{1,0:T(8,128)(2,1)}), bf16[256,256]{1,0:T(8,128)(2,1)}) %reduce-scatter.11.cloned.1.call-update) | async-done | bytes 131088 | tf_op jit(solution)/shard_map/reduce_scatter | solution.py:479
  749.4 1.6 convert_element_type.79
  751.0 116.3 %reduce-scatter.5.cloned.1.call-done = bf16[128,768]{1,0:T(8,128)(2,1)} async-done(((bf16[4096,768]{1,0:T(8,128)(2,1)}), bf16[128,768]{1,0:T(8,128)(2,1)}) %reduce-scatter.5.cloned.1.call-update) | async-done | bytes 196624 | tf_op jit(solution)/shard_map/reduce_scatter | solution.py:479
  867.3 1.7 convert_element_type.73
  (79 shorter events, 23.1 us)
Async XLA Ops:
  7.2 18.6 %copy-start = (bf16[128,1536]{1,0:T(8,128)(2,1)S(1)}, bf16[128,1536]{1,0:T(8,128)(2,1)}, u32[]{:S(2)}) copy-start(bf16[128,1536]{1,0:T(8,128)(2,1)} %param.13) | copy-start | bytes 1179652
  7.2 80.7 %all-gather.5.cloned.1.call-start = ((), (), s32[]{:S(2)}) async-start(), calls=%async_computation.7 | async-start | bytes 6488064 | tf_op jit(solution)/shard_map/all_gather | solution.py:471
  7.9 151.9 %all-gather.7.cloned.1.call-start = ((), (), s32[]{:S(2)}) async-start(), calls=%async_computation.8 | async-start | bytes 2162688 | tf_op jit(solution)/shard_map/all_gather | solution.py:471
  8.7 200.9 %all-gather.9.cloned.1.call-start = ((), (), s32[]{:S(2)}) async-start(), calls=%async_computation.9 | async-start | bytes 4325376 | tf_op jit(solution)/shard_map/all_gather | solution.py:471
  9.4 263.6 %all-gather.11.cloned.1.call-start = ((), (), s32[]{:S(2)}) async-start(), calls=%async_computation.10 | async-start | bytes 4325376 | tf_op jit(solution)/shard_map/all_gather | solution.py:471
  11.2 14.4 %all-to-all-start = ((s32[32,1,4]{2,1,0:T(1,128)}), s32[32,1,4]{2,1,0:T(1,128)S(1)}, u32[]{:S(2)}, u32[]{:S(2)}) async-start(s32[32,1,4]{2,1,0:T(1,128)} %broadcast_in_dim.27), calls=%async_computation | async-start | bytes 32768 | tf_op jit(solution)/shard_map/all_to_all | solution.py:498
  19.4 8.1 copy-start.6
  19.5 8.0 copy-start.8
  19.5 16.2 %copy-start.3 = (s32[1024]{0:T(1024)}, s32[1024]{0:T(1024)S(1)}, u32[]{:S(2)}) copy-start(s32[1024]{0:T(1024)S(1)} %convert_reduce_fusion.1) | copy-start | bytes 12292
  25.8 1.7 copy-start.4
  27.5 34.1 %all-to-all-start.1 = ((f32[32,4,1536]{2,1,0:T(4,128)}), f32[32,4,1536]{2,1,0:T(4,128)S(1)}, u32[]{:S(2)}, u32[]{:S(2)}) async-start(f32[32,4,1536]{2,1,0:T(4,128)} %reshape.424), calls=%async_computation.1 | async-start | bytes 1572864 | tf_op jit(solution)/shard_map/all_to_all | solution.py:509
  31.1 461.1 %reduce-scatter.7.cloned.1.call-start = ((), (), s32[]{:S(2)}) async-start(), calls=%async_computation.12 | async-start | bytes 2162688 | tf_op jit(solution)/shard_map/reduce_scatter | solution.py:479
  319.1 1.6 copy-start.10
  319.1 284.2 %reduce-scatter.9.cloned.1.call-start = ((), (), s32[]{:S(2)}) async-start(), calls=%async_computation.13 | async-start | bytes 4325376 | tf_op jit(solution)/shard_map/reduce_scatter | solution.py:479
  342.1 1.6 copy-start.12
  342.1 407.3 %reduce-scatter.11.cloned.1.call-start = ((), (), s32[]{:S(2)}) async-start(), calls=%async_computation.14 | async-start | bytes 4325376 | tf_op jit(solution)/shard_map/reduce_scatter | solution.py:479
  358.3 509.1 %reduce-scatter.5.cloned.1.call-start = ((), (), s32[]{:S(2)}) async-start(), calls=%async_computation.11 | async-start | bytes 6488064 | tf_op jit(solution)/shard_map/reduce_scatter | solution.py:479
  414.7 8.8 %copy-start.11 = (bf16[1024,1024]{1,0:T(8,128)(2,1)S(1)}, bf16[1024,1024]{1,0:T(8,128)(2,1)}, u32[]{:S(2)}) copy-start(bf16[1024,1024]{1,0:T(8,128)(2,1)} %get-tuple-element.31) | copy-start | bytes 6291460
  453.8 16.7 %copy-start.2 = (f32[8,4096]{1,0:T(8,128)S(1)}, f32[8,4096]{1,0:T(8,128)}, u32[]{:S(2)}) copy-start(f32[8,4096]{1,0:T(8,128)} %get-tuple-element.30) | copy-start | bytes 393220
  469.6 21.1 %copy-start.5 = (f32[128]{0:T(128)S(1)}, f32[128]{0:T(128)}, u32[]{:S(2)}) copy-start(f32[128]{0:T(128)} %copy-done.4) | copy-start | bytes 1540
  469.6 21.1 %copy-start.7 = (f32[128]{0:T(128)S(1)}, f32[128]{0:T(128)}, u32[]{:S(2)}) copy-start(f32[128]{0:T(128)} %copy-done.6) | copy-start | bytes 1540
  469.6 21.1 %copy-start.9 = (pred[128]{0:T(512)(128)(4,1)S(1)}, pred[128]{0:T(512)(128)(4,1)}, u32[]{:S(2)}) copy-start(pred[128]{0:T(512)(128)(4,1)} %copy-done.8) | copy-start | bytes 388
  470.7 398.4 %copy-start.1 = (bf16[128,1536]{1,0:T(8,128)(2,1)S(1)}, bf16[128,1536]{1,0:T(8,128)(2,1)}, u32[]{:S(2)}) copy-start(bf16[128,1536]{1,0:T(8,128)(2,1)} %param.13) | copy-start | bytes 1179652
Sparse Core Ops, SparseCore 0:
  10.9 76.9 all-gather.4
  90.9 54.9 all-gather.6
  149.0 60.5 all-gather.8
  212.5 60.4 all-gather.10
  319.2 137.8 reduce-scatter.6
  459.2 143.9 reduce-scatter.8
  605.6 143.7 reduce-scatter.10
  755.0 112.2 reduce-scatter.4

commit v2 on v1

--- a/solution.py
+++ b/solution.py
@@ -60,7 +60,7 @@
     )
 
 
-def project_kernel(clips, frames_ref, seg_ref, mod_ref, weight_ref, cos_ref, sin_ref, attn_ref, out_ref):
+def project_kernel(clips, frames_ref, seg_ref, mod_ref, weight_ref, cos_ref, sin_ref, turned_ref, out_ref, attn_ref):
     width = frames_ref.shape[1]
 
     @pl.when(pl.program_id(0) == 0)
@@ -71,7 +71,9 @@
             seg = seg_ref[r : r + step]
             shift = clip_rows(seg, mod_ref, 0, width, clips)
             scale = clip_rows(seg, mod_ref, 1, width, clips)
-            attn_ref[r : r + step] = (normed * (1.0 + scale) + shift).astype(BF16)
+            attn_in = (normed * (1.0 + scale) + shift).astype(BF16)
+            attn_ref[r : r + step] = attn_in
+            turned_ref[:, r : r + step] = attn_in.T
 
     result = dot_nn(attn_ref[...], weight_ref[0])
     for c in range(0, result.shape[1], LANES):
@@ -98,11 +100,12 @@
             pl.BlockSpec((1, count, LANES), lambda u: (u // per_part, 0, 0)),
         ],
         out_specs=[
-            pl.BlockSpec((count, width), whole),
+            pl.BlockSpec((width, count), whole),
             pl.BlockSpec((count, tile), lambda u: (0, u)),
         ],
+        scratch_shapes=[pltpu.VMEM((count, width), BF16)],
         out_shape=[
-            jax.ShapeDtypeStruct((count, width), BF16),
+            jax.ShapeDtypeStruct((width, count), BF16),
             jax.ShapeDtypeStruct((count, blocks * columns), BF16),
         ],
         compiler_params=pltpu.CompilerParams(vmem_limit_bytes=VMEM_LIMIT),
@@ -125,10 +128,10 @@
 
 
 def transposed(values):
-    return values.astype(F32).T.astype(BF16)
-
-
-def attend_kernel(single_ref, q_ref, k_ref, v_ref, segr_ref, segc_ref, out_ref, lse_ref, mixed):
+    return values.T
+
+
+def attend_kernel(single_ref, q_ref, k_ref, v_ref, segr_ref, segc_ref, out_ref, turned_ref, lse_ref, mixed):
     keys = k_ref[...]
     values_t = transposed(v_ref[...])
     count = keys.shape[0]
@@ -150,7 +153,9 @@
 
     pl.when(single_ref[0] == 1)(functools.partial(run, False))
     pl.when(single_ref[0] != 1)(functools.partial(run, True))
-    out_ref[...] = mixed[...].T.astype(BF16)
+    low = mixed[...].astype(BF16)
+    turned_ref[...] = low
+    out_ref[...] = low.T
 
 
 def attend_call(single, qkv, seg_row, seg_col):
@@ -172,12 +177,14 @@
             ],
             out_specs=[
                 block(0),
+                pl.BlockSpec((LANES, count), lambda p, s: (p, 0)),
                 pl.BlockSpec((1, LANES // HEAD_DIM, count), lambda p, s: (p, 0, 0)),
             ],
             scratch_shapes=[pltpu.VMEM((LANES, count), F32)],
         ),
         out_shape=[
             jax.ShapeDtypeStruct((count, width), BF16),
+            jax.ShapeDtypeStruct((width, count), BF16),
             jax.ShapeDtypeStruct((pairs, LANES // HEAD_DIM, count), F32),
         ],
         compiler_params=pltpu.CompilerParams(vmem_limit_bytes=VMEM_LIMIT),
@@ -190,8 +197,9 @@
 
 def attend_back_kernel(
     single_ref, q_ref, k_ref, v_ref, grad_ref, out_ref, lse_ref, segr_ref, segc_ref, cos_ref, sin_ref,
-    result_ref, grad_q, grad_k, grad_v,
+    *rest,
 ):
+    result_ref, grad_q, grad_k, grad_v = rest[-4:]
     keys = k_ref[...]
     values = v_ref[...]
     keys_t = transposed(keys)
@@ -234,30 +242,31 @@
     result_ref[2] = grad_v[...].astype(BF16)
 
 
-def attend_back_call(single, qkv, grad_mixed, attn_out, lse, seg_row, seg_col, cosine, sine):
+def attend_back_call(first, number, before, single, qkv, grad_mixed, attn_out, lse, seg_row, seg_col, cosine, sine):
     count, width = attn_out.shape
     pairs = width // LANES
     heads = LANES // HEAD_DIM
-    block = lambda t: pl.BlockSpec((count, LANES), lambda p, s: (0, t * pairs + p))
+    block = lambda t: pl.BlockSpec((count, LANES), lambda p, s: (0, t * pairs + first + p))
+    extra = [] if before is None else [before]
     fixed = lambda shape: pl.BlockSpec(shape, lambda p, s: (0, 0))
     return pl.pallas_call(
         attend_back_kernel,
         grid_spec=pltpu.PrefetchScalarGridSpec(
             num_scalar_prefetch=1,
-            grid=(pairs,),
+            grid=(number,),
             in_specs=[
                 block(0),
                 block(1),
                 block(2),
                 block(0),
                 block(0),
-                pl.BlockSpec((1, heads, count), lambda p, s: (p, 0, 0)),
+                pl.BlockSpec((1, heads, count), lambda p, s: (first + p, 0, 0)),
                 fixed((1, count)),
                 fixed((count, 1)),
                 fixed((count, LANES)),
                 fixed((count, LANES)),
-            ],
-            out_specs=pl.BlockSpec((3, count, LANES), lambda p, s: (0, 0, p)),
+            ] + [pl.BlockSpec(memory_space=pl.ANY)] * len(extra),
+            out_specs=pl.BlockSpec((3, count, LANES), lambda p, s: (0, 0, first + p)),
             scratch_shapes=[
                 pltpu.VMEM((LANES, count), F32),
                 pltpu.VMEM((count, LANES), F32),
@@ -267,61 +276,74 @@
         out_shape=jax.ShapeDtypeStruct((3, count, width), BF16),
         compiler_params=pltpu.CompilerParams(vmem_limit_bytes=VMEM_LIMIT),
         cost_estimate=pl.CostEstimate(
-            flops=40 * count * count * width, bytes_accessed=16 * count * width, transcendentals=16 * count * count
-        ),
+            flops=40 * count * count * LANES * number,
+            bytes_accessed=16 * count * LANES * number,
+            transcendentals=2 * count * count * number,
+        ),
+        input_output_aliases={11: 0} if extra else {},
         name="attend_back",
-    )(single, qkv, qkv, qkv, grad_mixed, attn_out, lse, seg_row, seg_col, cosine, sine)
-
-
-def by_columns(left, weight_ref):
-    return jnp.concatenate([dot_nn(left, weight_ref[b]) for b in range(weight_ref.shape[0])], axis=1)
-
-
-def by_rows(left, weight_ref):
-    columns = weight_ref.shape[2]
+    )(single, qkv, qkv, qkv, grad_mixed, attn_out, lse, seg_row, seg_col, cosine, sine, *extra)
+
+
+def by_columns(left, pieces):
+    return jnp.concatenate([dot_nn(left, piece) for piece in pieces], axis=1)
+
+
+def by_rows(left, pieces):
+    columns = pieces[0].shape[1]
     total = None
-    for b in range(weight_ref.shape[0]):
-        term = dot_nt(left[:, b * columns : (b + 1) * columns], weight_ref[b])
+    for b, piece in enumerate(pieces):
+        term = dot_nt(left[:, b * columns : (b + 1) * columns], piece)
         total = term if total is None else total + term
     return total
 
 
 def middle_kernel(
-    clips, frames_ref, cot_ref, attn_ref, seg_ref, member_ref, mod_ref, wo_ref, wu_ref, wd_ref,
+    clips, frames_ref, cot_ref, attn_ref, seg_ref, member_ref, mod_ref, weights_ref,
     block_ref, ffn_ref, hidden_ref, down_ref, up_ref, gmid_ref, gbranch_ref, gmixed_ref, sums_ref,
 ):
     width = frames_ref.shape[1]
     seg = seg_ref[...]
     member = member_ref[...]
     cot = cot_ref[...].astype(F32)
-    branch = by_columns(attn_ref[...], wo_ref)
+    blocks, parts, height, columns = weights_ref.shape
+    unit = height // 5
+
+    def piece(b, start, stop):
+        rows = weights_ref[b, :, start * unit : stop * unit, :]
+        return rows.reshape(parts * (stop - start) * unit, columns)
+
+    wo = [piece(b, 0, 1) for b in range(blocks)]
+    wu = [piece(b, 1 + j, 2 + j) for b in range(blocks) for j in range(2)]
+    wd = [piece(b, 3, 5) for b in range(blocks)]
+    branch = by_columns(attn_ref[...], wo)
     gate_one = clip_rows(seg, mod_ref, 2, width, clips)
     middle = frames_ref[...].astype(F32) + gate_one * branch
     normed, scale_n = norm_parts(middle)
     scale_two = 1.0 + clip_rows(seg, mod_ref, 4, width, clips)
     ffn_in = (normed * scale_two + clip_rows(seg, mod_ref, 3, width, clips)).astype(BF16)
-    ffn_ref[...] = ffn_in
-    upward = by_columns(ffn_in, wu_ref)
+    ffn_ref[...] = ffn_in.T
+    upward = by_columns(ffn_in, wu)
     root = math.sqrt(2.0 / math.pi)
     square = upward * upward
     wave = jnp.tanh(root * upward * (1.0 + 0.044715 * square))
     half = 0.5 * (1.0 + wave)
     hidden = (upward * half).astype(BF16)
-    hidden_ref[...] = hidden
+    hidden_ref[...] = hidden.T
     slope = half + 0.5 * upward * (1.0 - wave * wave) * (root * (1.0 + 3.0 * 0.044715 * square))
-    downward = by_columns(hidden, wd_ref)
+    downward = by_columns(hidden, wd)
     gate_two = clip_rows(seg, mod_ref, 5, width, clips)
     block_ref[...] = (middle + gate_two * downward).astype(BF16)
     grad_down = (gate_two * cot).astype(BF16)
     down_ref[...] = grad_down
-    grad_up = (by_rows(grad_down, wd_ref) * slope).astype(BF16)
+    grad_up = (by_rows(grad_down, wd) * slope).astype(BF16)
     up_ref[...] = grad_up
-    grad_ffn = by_rows(grad_up, wu_ref)
+    grad_ffn = by_rows(grad_up, wu)
     grad_middle = cot + norm_back(grad_ffn * scale_two, normed, scale_n)
     gmid_ref[...] = grad_middle
     grad_branch = (gate_one * grad_middle).astype(BF16)
     gbranch_ref[...] = grad_branch
-    gmixed_ref[...] = by_rows(grad_branch, wo_ref).astype(BF16)
+    gmixed_ref[...] = by_rows(grad_branch, wo).astype(BF16)
 
     @pl.when(pl.program_id(0) == 0)
     def _():
@@ -333,13 +355,13 @@
         sums_ref[:, i * width : (i + 1) * width] += clip_sums(member, values)
 
 
-def middle_call(frames, cotangent, attn_out, seg_col, member, mod, wo, wu, wd, clips):
+def middle_call(frames, cotangent, attn_out, seg_col, member, mod, weights, clips):
     count, width = frames.shape
-    hidden = wd.shape[1]
+    hidden = 2 * width
     tile = 256
     rows = lambda w: pl.BlockSpec((tile, w), lambda i: (i, 0))
     fixed2 = lambda a: pl.BlockSpec(a.shape, lambda i: (0, 0))
-    held = lambda a: pl.BlockSpec(a.shape, lambda i: (0, 0, 0), pipeline_mode=pl.Buffered(1))
+    turned = lambda h: pl.BlockSpec((h, tile), lambda i: (0, i))
     shape = lambda w, t: jax.ShapeDtypeStruct((count, w), t)
     return pl.pallas_call(
         functools.partial(middle_kernel, clips),
@@ -351,14 +373,12 @@
             rows(1),
             pl.BlockSpec((member.shape[0], tile), lambda i: (0, i)),
             fixed2(mod),
-            held(wo),
-            held(wu),
-            held(wd),
+            pl.BlockSpec(weights.shape, lambda i: (0, 0, 0, 0), pipeline_mode=pl.Buffered(1)),
         ],
         out_specs=[
             rows(width),
-            rows(width),
-            rows(hidden),
+            turned(width),
+            turned(hidden),
             rows(width),
             rows(hidden),
             rows(width),
@@ -368,8 +388,8 @@
         ],
         out_shape=[
             shape(width, BF16),
-            shape(width, BF16),
-            shape(hidden, BF16),
+            jax.ShapeDtypeStruct((width, count), BF16),
+            jax.ShapeDtypeStruct((hidden, count), BF16),
             shape(width, BF16),
             shape(hidden, BF16),
             shape(width, F32),
@@ -384,7 +404,7 @@
             transcendentals=count * hidden,
         ),
         name="middle",
-    )(frames, cotangent, attn_out, seg_col, member, mod, wo, wu, wd)
+    )(frames, cotangent, attn_out, seg_col, member, mod, weights)
 
 
 def tail_kernel(clips, frames_ref, gmid_ref, gp_ref, seg_ref, member_ref, mod_ref, wp_ref, out_ref, sums_ref):
@@ -472,11 +492,108 @@
     return full.reshape(blocks, full.shape[0] // blocks, full.shape[1])
 
 
-def scatter_blocks(left, right, blocks):
-    local = lax.dot_general(left, right, (((0,), (0,)), ((), ())), preferred_element_type=F32).astype(BF16)
-    rows = local.shape[0]
-    local = local.reshape(rows, blocks, -1).transpose(1, 0, 2).reshape(blocks * rows, -1)
-    return lax.psum_scatter(local, AXES, scatter_dimension=0, tiled=True).astype(F32)
+def unit_kernel(order_ref, left_ref, right_ref, out_ref):
+    out_ref[0] = dot_nn(left_ref[...], right_ref[0]).astype(BF16)
+
+
+def unit_products(order, left, right, tile):
+    rows, count = left.shape
+    number = order.shape[0]
+    per_part = right.shape[2] // tile
+    return pl.pallas_call(
+        unit_kernel,
+        grid_spec=pltpu.PrefetchScalarGridSpec(
+            num_scalar_prefetch=1,
+            grid=(number,),
+            in_specs=[
+                pl.BlockSpec((rows, count), lambda i, o: (0, 0)),
+                pl.BlockSpec((1, count, tile), lambda i, o: (o[i] // per_part, 0, o[i] % per_part)),
+            ],
+            out_specs=pl.BlockSpec((1, rows, tile), lambda i, o: (i, 0, 0)),
+        ),
+        out_shape=jax.ShapeDtypeStruct((number, rows, tile), BF16),
+        compiler_params=pltpu.CompilerParams(vmem_limit_bytes=VMEM_LIMIT),
+        cost_estimate=pl.CostEstimate(
+            flops=2 * number * rows * count * tile,
+            bytes_accessed=2 * (rows * count + number * tile * (rows + count)),
+            transcendentals=0,
+        ),
+        name="unit_products",
+    )(order, left, right)
+
+
+def pair_kernel(attn_ref, ffn_ref, branch_ref, up_ref, out_ref):
+    parts, height, tile = out_ref.shape[1:]
+
+    @pl.when(pl.program_id(1) == 0)
+    def _():
+        out_ref[0] = dot_nn(attn_ref[...], branch_ref[...]).astype(BF16).reshape(parts, height, tile)
+
+    @pl.when(pl.program_id(1) != 0)
+    def _():
+        out_ref[0] = dot_nn(ffn_ref[...], up_ref[...]).astype(BF16).reshape(parts, height, tile)
+
+
+def pair_products(blocks, parts, tile, attn_t, ffn_t, grad_branch, grad_up):
+    width, count = attn_t.shape
+    height = width // parts
+    fixed = pl.BlockSpec((width, count), lambda b, k: (0, 0))
+    return pl.pallas_call(
+        pair_kernel,
+        grid=(blocks, 3),
+        in_specs=[
+            fixed,
+            fixed,
+            pl.BlockSpec((count, tile), lambda b, k: (0, b)),
+            pl.BlockSpec((count, tile), lambda b, k: (0, 2 * b + jnp.maximum(k - 1, 0))),
+        ],
+        out_specs=pl.BlockSpec((1, parts, height, tile), lambda b, k: (b, 0, k, 0)),
+        out_shape=jax.ShapeDtypeStruct((blocks, parts, 3 * height, tile), BF16),
+        compiler_params=pltpu.CompilerParams(vmem_limit_bytes=VMEM_LIMIT),
+        cost_estimate=pl.CostEstimate(
+            flops=6 * blocks * tile * width * count, bytes_accessed=16 * count * width, transcendentals=0
+        ),
+        name="pair_products",
+    )(attn_t, ffn_t, grad_branch, grad_up)
+
+
+def halve(send, keep, stages, sizes):
+    live = [("dp", b) for b in range(1, sizes["dp"].bit_length() - 1)]
+    live += [("fsdp", b) for b in reversed(range(sizes["fsdp"].bit_length() - 1))]
+
+    def exchange(values, axis, bit):
+        return lax.ppermute(values, axis, [(i, i ^ (1 << bit)) for i in range(sizes[axis])])
+
+    got = exchange(send, "dp", 0)
+    for axis, bit in stages:
+        at = live.index((axis, bit))
+        live.pop(at)
+        mine = 1 if axis == "dp" else (lax.axis_index(axis) >> bit) & 1
+
+        def side(which):
+            pick = lambda v: lax.dynamic_index_in_dim(v, which, at, keepdims=False).astype(F32)
+            return pick(keep) + pick(got)
+
+        send, keep = side(1 - mine).astype(BF16), side(mine)
+        got = exchange(send, axis, bit)
+    return keep.astype(F32) + got.astype(F32)
+
+
+def stage_orders(sizes):
+    dp = [("dp", b) for b in range(1, sizes["dp"].bit_length() - 1)]
+    fsdp = [("fsdp", b) for b in range(sizes["fsdp"].bit_length() - 1)]
+    return (dp + fsdp, fsdp[:1] + dp + fsdp[1:], fsdp[1:] + dp + fsdp[:1])
+
+
+def near_order(blocks, lowest):
+    bits = blocks.bit_length() - 1
+    flips = []
+    for place in range(blocks // 2):
+        flip = 1 - lowest
+        for b in range(1, bits):
+            flip |= (1 - ((place >> (bits - 1 - b)) & 1)) << b
+        flips.append(flip)
+    return lax.axis_index("dp") ^ jnp.array(flips, jnp.int32)
 
 
 def per_device(
@@ -511,30 +628,56 @@
     mod = mod.transpose(1, 0, 2).reshape(clips, blocks * columns)
     mod = jnp.pad(mod, ((0, pad), (0, 0)))
 
-    wo = gather_blocks(output_weight, blocks)
-    wu = gather_blocks(upward_weight, blocks)
-    wd = gather_blocks(downward_weight, blocks)
+    tile = output_weight.shape[1]
+    shard = jnp.concatenate(
+        [output_weight, upward_weight[:, :tile], upward_weight[:, tile:], downward_weight], axis=0
+    )
+    weights = lax.all_gather(shard, AXES, axis=0, tiled=True).reshape(blocks, row_parts, shard.shape[0], tile)
 
     scale = HEAD_DIM ** -0.5
     one = jnp.ones_like(cosine)
-    attn_in, qkv = project_call(
+    attn_in_t, qkv = project_call(
         frames, seg_col, mod, wp,
         jnp.stack([cosine * scale, cosine, one]),
         jnp.stack([sine * scale, sine, 0.0 * one]),
         clips,
     )
-    attn_out, lse = attend_call(single, qkv, seg_row, seg_col)
-    block_out, ffn_in, hidden, grad_down, grad_up, grad_middle, grad_branch, grad_mixed, sums_two = middle_call(
-        frames, cotangent, attn_out, seg_col, member, mod, wo, wu, wd, clips
-    )
-    downward_grad = scatter_blocks(hidden, grad_down, blocks)
-    upward_grad = scatter_blocks(ffn_in, grad_up, blocks)
-    output_grad = scatter_blocks(attn_out, grad_branch, blocks)
-    grad_projected = attend_back_call(
-        single, qkv, grad_mixed, attn_out, lse, seg_row, seg_col, cosine, sine
-    )
-    flat = grad_projected.transpose(1, 0, 2).reshape(count, 3 * width)
-    project_grad = scatter_blocks(attn_in, flat, blocks)
+    attn_out, attn_t, lse = attend_call(single, qkv, seg_row, seg_col)
+    block_out, ffn_t, hidden_t, grad_down, grad_up, grad_middle, grad_branch, grad_mixed, sums_two = middle_call(
+        frames, cotangent, attn_out, seg_col, member, mod, weights, clips
+    )
+
+    sizes = {"dp": blocks, "fsdp": row_parts}
+    orders = stage_orders(sizes)
+    bits = (2,) * (blocks.bit_length() - 2 + row_parts.bit_length() - 1)
+    far, near = near_order(blocks, 0), near_order(blocks, 1)
+
+    down_send = unit_products(far, hidden_t, grad_down[None], tile)
+    down_keep = unit_products(near, hidden_t, grad_down[None], tile)
+    shape = bits + downward_weight.shape
+    downward_grad = halve(down_send.reshape(shape), down_keep.reshape(shape), orders[1], sizes)
+
+    pair = pair_products(blocks, row_parts, tile, attn_t, ffn_t, grad_branch, grad_up)
+    pair = lax.psum_scatter(pair.reshape(-1, tile), AXES, scatter_dimension=0, tiled=True).astype(F32)
+    output_grad, upward_left, upward_right = jnp.split(pair, 3, axis=0)
+    upward_grad = jnp.concatenate([upward_left, upward_right], axis=1)
+
+    grad_projected = None
+    number = width // LANES // 2
+    for first in (0, number):
+        grad_projected = attend_back_call(
+            first, number, grad_projected,
+            single, qkv, grad_mixed, attn_out, lse, seg_row, seg_col, cosine, sine,
+        )
+    units = project_weight.shape[1] // tile
+    shape = bits + (project_weight.shape[0], tile)
+    sends = [unit_products(far * units + j, attn_in_t, grad_projected, tile) for j in range(units)]
+    keeps = unit_products(
+        jnp.concatenate([near * units + j for j in range(units)]), attn_in_t, grad_projected, tile
+    ).reshape((units,) + shape)
+    project_grad = jnp.concatenate(
+        [halve(sends[j].reshape(shape), keeps[j], orders[j % 3], sizes) for j in range(units)], axis=1
+    )
     frames_grad, sums_one = tail_call(
         frames, grad_middle, grad_projected, seg_col, member, mod, wp, clips
     )

time: 886 us -> 464 us (0.52)
  waiting for transfers between devices: 537 us -> 105 us
  Pallas kernels: 182 us -> 237 us
  matrix products: 35.2 us -> 2.02 us
  local copies, waits for them, and re-layouts: 57.4 us -> 25.5 us
  starting transfers between devices: 11.2 us -> 42.8 us
  blocking collectives: 19.9 us -> 0 us
  other arithmetic: 18.2 us -> 28 us
    reduce_scatter x4 -> x1, waiting for transfers between devices: 370 us -> 0.01 us  [per_device(): lax.psum_scatter(pair.reshape(-1, tile), AXES, scatter_dimension=0, tiled...]
    all_gather x4 -> x1, waiting for transfers between devices: 139 us -> 24.5 us  [gather_blocks(): full = lax.all_gather(weight, AXES, axis=0, tiled=True)]
    pallas_call x0 -> x7, Pallas kernels: none -> 51.3 us  [the longest x6 36.5 us: unit_products(): pl.pallas_call(unit_kernel, grid_spec=pltpu.PrefetchScalarGridSpec(num_sc...]
    ppermute x0 -> x20, waiting for transfers between devices: none -> 44.7 us  [exchange(): lax.ppermute(values, axis, [(i, i ^ 1 << bit) for i in range(sizes[axis])])]
    dot_general x4 -> x0, matrix products: 33.1 us -> none  [scatter_blocks(): lax.dot_general(left, right, (((0,), (0,)), ((), ())), preferred_element_...]
    transpose x5 -> x0, local copies, waits for them, and re-layouts: 28.9 us -> none  [the longest x4 20.1 us: scatter_blocks(): local.reshape(rows, blocks, -1).transpose(1, 0, 2)]
    ppermute x0 -> x20, starting transfers between devices: none -> 26.8 us  [exchange(): lax.ppermute(values, axis, [(i, i ^ 1 << bit) for i in range(sizes[axis])])]
    all_to_all x1 -> x0, blocking collectives: 19.9 us -> none  [per_device(): lax.all_to_all(grad_mod.reshape(devices, clips, columns), AXES, 0, 0, til...]
  transfers between devices with their start and end apart: 10 -> 26, of which waited for: 8 -> 12; matrix products, arithmetic and copies ran while one was open for 11% -> 11% of each run, Pallas kernels for 16% -> 42%
where the time goes in v2:
time: 464 us; the launch traced here: 456 us
  Pallas kernels  237 us (51%)
  waiting for transfers between devices  105 us (23%)
  starting transfers between devices  42.8 us (9%)
  other arithmetic  28 us (6%)
  local copies, waits for them, and re-layouts  25.5 us (5%)
  between operations  15.8 us (3%)
    pallas_call x2, Pallas kernels, attend_back_call(): pl.pallas_call(attend_back_kernel, grid_spec=pltpu.PrefetchScalarGridSpec...  58.2 us
    pallas_call x1, Pallas kernels, attend_call(): pl.pallas_call(attend_kernel, grid_spec=pltpu.PrefetchScalarGridSpec(num_...  50.5 us
    ppermute x20, waiting for transfers between devices, exchange(): lax.ppermute(values, axis, [(i, i ^ 1 << bit) for i in range(sizes[axis])])  44.7 us
    pallas_call x1, Pallas kernels, middle_call(): pl.pallas_call(functools.partial(middle_kernel, clips), grid=(count // ti...  39.4 us
    pallas_call x6, Pallas kernels, unit_products(): pl.pallas_call(unit_kernel, grid_spec=pltpu.PrefetchScalarGridSpec(num_sc...  36.5 us
    ppermute x20, starting transfers between devices, exchange(): lax.ppermute(values, axis, [(i, i ^ 1 << bit) for i in range(sizes[axis])])  26.8 us
    all_gather x1, waiting for transfers between devices, gather_blocks(): full = lax.all_gather(weight, AXES, axis=0, tiled=True)  24.5 us
    pallas_call x1, Pallas kernels, project_call(): pl.pallas_call(functools.partial(project_kernel, clips), grid=(blocks * p...  21.4 us
  transfers between devices with their start and end apart: 26, of which 12 were waited for; matrix products, arithmetic and copies ran while one was open for 11% of the time, Pallas kernels for 42%

profile of v2, /device:TPU:0, one launch (start us, length us, event | category | flops | bytes accessed | tf_op | source)
XLA Modules:
  0.0 456.0 jit_solution(10054693979605052244)
XLA Ops:
  11.8 7.3 %all-to-all-start = ((s32[32,1,4]{2,1,0:T(1,128)}), s32[32,1,4]{2,1,0:T(1,128)S(1)}, u32[]{:S(2)}, u32[]{:S(2)}) async-start(s32[32,1,4]{2,1,0:T(1,128)} %broadcast_in_dim.32), calls=%async_computation | async-start | bytes 32768 | tf_op jit(solution)/shard_map/all_to_all | solution.py:615
  22.6 3.0 fusion.25
  28.0 5.3 %all-to-all-start.1 = ((f32[32,4,1536]{2,1,0:T(4,128)}), f32[32,4,1536]{2,1,0:T(4,128)S(1)}, u32[]{:S(2)}, u32[]{:S(2)}) async-start(f32[32,4,1536]{2,1,0:T(4,128)} %reshape.531), calls=%async_computation.1 | async-start | bytes 1572864 | tf_op jit(solution)/shard_map/all_to_all | solution.py:626
  36.5 3.8 pad_maximum_fusion
  45.0 18.6 %all-to-all-done.1 = f32[32,4,1536]{2,1,0:T(4,128)S(1)} async-done(((f32[32,4,1536]{2,1,0:T(4,128)}), f32[32,4,1536]{2,1,0:T(4,128)S(1)}, u32[]{:S(2)}, u32[]{:S(2)}) %all-to-all-start.1) | async-done | bytes 786464 | tf_op jit(solution)/shard_map/all_to_all | solution.py:626
  64.4 24.5 %all-gather.3.cloned.1.call-done = bf16[4096,768]{1,0:T(8,128)(2,1)} async-done(((bf16[128,768]{1,0:T(8,128)(2,1)}), bf16[4096,768]{1,0:T(8,128)(2,1)}) %all-gather.3.cloned.1.call-update) | async-done | bytes 6291472 | tf_op jit(solution)/shard_map/all_gather | solution.py:491
  88.9 21.4 %project.1 = (bf16[1024,1024]{1,0:T(8,128)(2,1)}, bf16[1024,3072]{1,0:T(8,128)(2,1)}) custom-call(bf16[1024,1024]{1,0:T(8,128)(2,1)} %frames_ref.5, s32[1024,1]{1,0:T(8,128)} %copy.70.seg_ref.segc_ref, f32[8,6144]{1,0:T(8,128)} %pad.4.mod_ref, bf16[4,1024,768]{2,1,0:T(8,128)(2,1)} %bitcast.221, f32[3,1024,128]{2,1,0:T(8,128)} %maximum_maximum_fusion.cos_ref, ...), custom_call_target="tpu_custom_call" | custom-call | flops 6442450944 | bytes 16777216 | tf_op jit(solution)/shard_map/project/pallas_call | solution.py:91
  110.3 50.5 %attend.1 = (bf16[1024,1024]{1,0:T(8,128)(2,1)}, bf16[1024,1024]{1,0:T(8,128)(2,1)}, f32[8,2,1024]{2,1,0:T(2,128)}) custom-call(s32[1]{0:T(128)S(6)} %convert_element_type.317.single_ref, bf16[1024,3072]{1,0:T(8,128)(2,1)} %get-tuple-element.23.q_ref.k_ref.v_ref, bf16[1024,3072]{1,0:T(8,128)(2,1)} %get-tuple-element.23.q_ref.k_ref.v_ref, ...), custom_call_target="tpu_custom_call" | custom-call | flops 17179869184 | bytes 8388608 | tf_op jit(solution)/shard_map/attend/pallas_call | solution.py:166
  160.8 16.3 %all-gather.5.cloned.1.call-done = bf16[20480,256]{1,0:T(8,128)(2,1)} async-done(((bf16[640,256]{1,0:T(8,128)(2,1)}), bf16[20480,256]{1,0:T(8,128)(2,1)}) %all-gather.5.cloned.1.call-update) | async-done | bytes 10485776 | tf_op jit(solution)/shard_map/all_gather | solution.py:635
  177.1 39.4 %middle.1 = (bf16[1024,1024]{1,0:T(8,128)(2,1)}, bf16[1024,1024]{1,0:T(8,128)(2,1)}, bf16[2048,1024]{1,0:T(8,128)(2,1)}, bf16[1024,1024]{1,0:T(8,128)(2,1)}, bf1...) custom-call(bf16[1024,1024]{1,0:T(8,128)(2,1)} %frames_ref.5, ...), custom_call_target="tpu_custom_call" | custom-call | flops 21474836480 | bytes 41943040 | tf_op jit(solution)/shard_map/middle/pallas_call | solution.py:366
  216.5 6.6 %unit_products.11 = bf16[2,2048,256]{2,1,0:T(8,128)(2,1)} custom-call(s32[2]{0:T(128)} %get-tuple-element.86.order_ref, bf16[2048,1024]{1,0:T(8,128)(2,1)} %get-tuple-element.37.left_ref, bf16[1,1024,1024]{2,1,0:T(8,128)(2,1)} %bitcast.202), custom_call_target="tpu_custom_call" | custom-call | flops 2147483648 | bytes 7340032 | tf_op jit(solution)/shard_map/unit_products/pallas_call | solution.py:503
  223.1 3.1 copy.87
  226.5 14.9 %pair_products.1 = bf16[4,8,384,256]{3,2,1,0:T(8,128)(2,1)} custom-call(bf16[1024,1024]{1,0:T(8,128)(2,1)} %get-tuple-element.33.attn_ref, bf16[1024,1024]{1,0:T(8,128)(2,1)} %get-tuple-element.34.ffn_ref, bf16[1024,1024]{1,0:T(8,128)(2,1)} %get-tuple-element.35.branch_ref, bf16[1024,2048]{1,0:T(8,128)(2,1)} %get-tuple-element.36.up_ref), custom_call_target="tpu_custom_call" | custom-call | flops 6442450944 | bytes 16777216 | tf_op jit(solution)/shard_map/pair_products/pallas_call | solution.py:541
  241.3 29.0 %attend_back.2.rest_0_ = bf16[3,1024,1024]{2,1,0:T(8,128)(2,1)} custom-call(s32[1]{0:T(128)S(6)} %convert_element_type.317.single_ref, bf16[1024,3072]{1,0:T(8,128)(2,1)} %get-tuple-element.23.q_ref.k_ref.v_ref, bf16[1024,3072]{1,0:T(8,128)(2,1)} %get-tuple-element.23.q_ref.k_ref.v_ref, bf16[1024,3072]{1,0:T(8,128)(2,1)} %get-tuple-element.23.q_ref.k_ref.v_ref, ...), custom_call_target="tpu_custom_call" | custom-call | flops 21474836480 | bytes 8388608 | tf_op jit(solution)/shard_map/attend_back/pallas_call | solution.py:252
  270.4 29.2 %attend_back.3.gp_ref.right_ref = bf16[3,1024,1024]{2,1,0:T(8,128)(2,1)} custom-call(s32[1]{0:T(128)S(6)} %convert_element_type.317.single_ref, bf16[1024,3072]{1,0:T(8,128)(2,1)} %get-tuple-element.23.q_ref.k_ref.v_ref, bf16[1024,3072]{1,0:T(8,128)(2,1)} %get-tuple-element.23.q_ref.k_ref.v_ref, ...), custom_call_target="tpu_custom_call", output_to_operand_aliasing={{}: (11, {})} | custom-call | flops 21474836480 | bytes 8388608 | tf_op jit(solution)/shard_map/attend_back/pallas_call | solution.py:252
  299.5 4.7 %unit_products.7 = bf16[2,1024,256]{2,1,0:T(8,128)(2,1)} custom-call(s32[2]{0:T(128)} %get-tuple-element.89.order_ref, bf16[1024,1024]{1,0:T(8,128)(2,1)} %get-tuple-element.32.left_ref, bf16[3,1024,1024]{2,1,0:T(8,128)(2,1)} %attend_back.3.gp_ref.right_ref), custom_call_target="tpu_custom_call" | custom-call | flops 1073741824 | bytes 4194304 | tf_op jit(solution)/shard_map/unit_products/pallas_call | solution.py:503
  304.3 2.3 copy.77
  306.9 5.0 %unit_products.8 = bf16[2,1024,256]{2,1,0:T(8,128)(2,1)} custom-call(s32[2]{0:T(128)} %get-tuple-element.87.order_ref, bf16[1024,1024]{1,0:T(8,128)(2,1)} %get-tuple-element.32.left_ref, bf16[3,1024,1024]{2,1,0:T(8,128)(2,1)} %attend_back.3.gp_ref.right_ref), custom_call_target="tpu_custom_call" | custom-call | flops 1073741824 | bytes 4194304 | tf_op jit(solution)/shard_map/unit_products/pallas_call | solution.py:503
  314.4 4.8 %unit_products.9 = bf16[2,1024,256]{2,1,0:T(8,128)(2,1)} custom-call(s32[2]{0:T(128)} %get-tuple-element.88.order_ref, bf16[1024,1024]{1,0:T(8,128)(2,1)} %get-tuple-element.32.left_ref, bf16[3,1024,1024]{2,1,0:T(8,128)(2,1)} %attend_back.3.gp_ref.right_ref), custom_call_target="tpu_custom_call" | custom-call | flops 1073741824 | bytes 4194304 | tf_op jit(solution)/shard_map/unit_products/pallas_call | solution.py:503
  319.2 2.4 copy.84
  321.8 15.7 %tail.1 = (f32[1024,1024]{1,0:T(8,128)}, f32[8,2048]{1,0:T(8,128)}) custom-call(bf16[1024,1024]{1,0:T(8,128)(2,1)} %frames_ref.5, f32[1024,1024]{1,0:T(8,128)} %get-tuple-element.26.gmid_ref, bf16[3,1024,1024]{2,1,0:T(8,128)(2,1)} %attend_back.3.gp_ref.right_ref, s32[1024,1]{1,0:T(8,128)} %copy.70.seg_ref.segc_ref, bf16[8,1024]{1,0:T(8,128)(2,1)} %fusion.45.member_ref, ...), custom_call_target="tpu_custom_call" | custom-call | flops 6442450944 | bytes 23068672 | tf_op jit(solution)/shard_map/tail/pallas_call | solution.py:438
  339.3 3.3 all-to-all-start.2
  342.7 8.8 %unit_products.6 = bf16[6,1024,256]{2,1,0:T(8,128)(2,1)} custom-call(s32[6]{0:T(128)} %pad_add_fusion.order_ref, bf16[1024,1024]{1,0:T(8,128)(2,1)} %get-tuple-element.32.left_ref, bf16[3,1024,1024]{2,1,0:T(8,128)(2,1)} %attend_back.3.gp_ref.right_ref), custom_call_target="tpu_custom_call" | custom-call | flops 3221225472 | bytes 8388608 | tf_op jit(solution)/shard_map/unit_products/pallas_call | solution.py:503
  353.7 6.6 %unit_products.10 = bf16[2,2048,256]{2,1,0:T(8,128)(2,1)} custom-call(s32[2]{0:T(128)} %get-tuple-element.90.order_ref, bf16[2048,1024]{1,0:T(8,128)(2,1)} %get-tuple-element.37.left_ref, bf16[1,1024,1024]{2,1,0:T(8,128)(2,1)} %bitcast.203), custom_call_target="tpu_custom_call" | custom-call | flops 2147483648 | bytes 7340032 | tf_op jit(solution)/shard_map/unit_products/pallas_call | solution.py:503
  377.5 3.6 collective-permute-done.1
  389.3 2.5 collective-permute-start.12
  391.8 20.4 %collective-permute-done.2 = bf16[2,2,128,256]{3,2,0,1:T(8,128)(2,1)S(1)} collective-permute-done((bf16[2,2,128,256]{3,2,0,1:T(8,128)(2,1)S(1)}, bf16[2,2,128,256]{3,2,0,1:T(8,128)(2,1)S(1)}, u32[]{:S(2)}, u32[]{:S(2)}) %collective-permute-start.2) | collective-permute-done | bytes 262176 | tf_op jit(solution)/shard_map/ppermute | solution.py:565
  418.0 2.9 collective-permute-start.4
  422.7 7.2 %collective-permute-done.13 = bf16[2,128,256]{2,1,0:T(8,128)(2,1)S(1)} collective-permute-done((bf16[2,128,256]{2,1,0:T(8,128)(2,1)S(1)}, bf16[2,128,256]{2,1,0:T(8,128)(2,1)S(1)}, u32[]{:S(2)}, u32[]{:S(2)}) %collective-permute-start.13) | collective-permute-done | bytes 131104 | tf_op jit(solution)/shard_map/ppermute | solution.py:565
  433.2 4.8 %collective-permute-done.18 = bf16[2,256,256]{2,1,0:T(8,128)(2,1)S(1)} collective-permute-done((bf16[2,256,256]{2,1,0:T(8,128)(2,1)S(1)}, bf16[2,256,256]{2,1,0:T(8,128)(2,1)S(1)}, u32[]{:S(2)}, u32[]{:S(2)}) %collective-permute-start.18) | collective-permute-done | bytes 262176 | tf_op jit(solution)/shard_map/ppermute | solution.py:565
  438.0 3.6 collective-permute-start.19
  442.4 3.5 collective-permute-done.19
  (124 shorter events, 65.2 us)
Async XLA Ops:
  7.2 19.2 %copy-start = (bf16[128,1536]{1,0:T(8,128)(2,1)S(1)}, bf16[128,1536]{1,0:T(8,128)(2,1)}, u32[]{:S(2)}) copy-start(bf16[128,1536]{1,0:T(8,128)(2,1)} %param.15) | copy-start | bytes 1179652
  7.2 81.7 %all-gather.3.cloned.1.call-start = ((), (), s32[]{:S(2)}) async-start(), calls=%async_computation.4 | async-start | bytes 6488064 | tf_op jit(solution)/shard_map/all_gather | solution.py:491
  7.9 169.1 %all-gather.5.cloned.1.call-start = ((), (), s32[]{:S(2)}) async-start(), calls=%async_computation.5 | async-start | bytes 10813440 | tf_op jit(solution)/shard_map/all_gather | solution.py:635
  11.8 14.4 %all-to-all-start = ((s32[32,1,4]{2,1,0:T(1,128)}), s32[32,1,4]{2,1,0:T(1,128)S(1)}, u32[]{:S(2)}, u32[]{:S(2)}) async-start(s32[32,1,4]{2,1,0:T(1,128)} %broadcast_in_dim.32), calls=%async_computation | async-start | bytes 32768 | tf_op jit(solution)/shard_map/all_to_all | solution.py:615
  20.1 21.7 %copy-start.7 = (s32[1024]{0:T(1024)}, s32[1024]{0:T(1024)S(1)}, u32[]{:S(2)}) copy-start(s32[1024]{0:T(1024)S(1)} %convert_reduce_fusion.1) | copy-start | bytes 12292
  28.0 35.6 %all-to-all-start.1 = ((f32[32,4,1536]{2,1,0:T(4,128)}), f32[32,4,1536]{2,1,0:T(4,128)S(1)}, u32[]{:S(2)}, u32[]{:S(2)}) async-start(f32[32,4,1536]{2,1,0:T(4,128)} %reshape.531), calls=%async_computation.1 | async-start | bytes 1572864 | tf_op jit(solution)/shard_map/all_to_all | solution.py:626
  33.4 413.4 %reduce-scatter.2.cloned.1.call-start = ((), (), s32[]{:S(2)}) async-start(), calls=%async_computation.6 | async-start | bytes 6488064 | tf_op jit(solution)/shard_map/reduce_scatter | solution.py:661
  226.2 145.7 %collective-permute-start.15 = (bf16[2,2,2,2,256,256]{5,4,1,2,3,0:T(8,128)(2,1)}, bf16[2,2,2,2,256,256]{5,4,1,2,3,0:T(8,128)(2,1)}, u32[]{:S(2)}, u32[]{:S(2)}) collective-permute-start(bf16[2,2,2,2,256,256]{5,4,1,2,3,0:T(8,128)(2,1)} %copy.87), channel_id=1, source_target_pairs={{0,8},{8,0},{16,24},{24,16},{1,9},{9,1},{17,25},{25,17},{2,10},{10... | collective-permute-start | bytes 6291464 | tf_op jit(solution)/shard_map/ppermute | solution.py:565
  306.6 58.6 %collective-permute-start = (bf16[2,2,2,2,128,256]{5,4,1,2,3,0:T(8,128)(2,1)}, bf16[2,2,2,2,128,256]{5,4,1,2,3,0:T(8,128)(2,1)}, u32[]{:S(2)}, u32[]{:S(2)}) collective-permute-start(bf16[2,2,2,2,128,256]{5,4,1,2,3,0:T(8,128)(2,1)} %copy.77), channel_id=1, source_target_pairs={{0,8},{8,0},{16,24},{24,16},{1,9},{9,1},{17,25},{25,17},{2,10},{10... | collective-permute-start | bytes 3145736 | tf_op jit(solution)/shard_map/ppermute | solution.py:565
  314.2 54.7 %collective-permute-start.5 = (bf16[2,2,2,2,128,256]{5,4,1,2,3,0:T(8,128)(2,1)}, bf16[2,2,2,2,128,256]{5,4,1,2,3,0:T(8,128)(2,1)}, u32[]{:S(2)}, u32[]{:S(2)}) collective-permute-start(bf16[2,2,2,2,128,256]{5,4,1,2,3,0:T(8,128)(2,1)} %copy.81), channel_id=1, source_target_pairs={{0,8},{8,0},{16,24},{24,16},{1,9},{9,1},{17,25},{25,17},{2,10},{10... | collective-permute-start | bytes 3145736 | tf_op jit(solution)/shard_map/ppermute | solution.py:565
  321.5 53.0 %collective-permute-start.10 = (bf16[2,2,2,2,128,256]{5,4,3,1,0,2:T(8,128)(2,1)}, bf16[2,2,2,2,128,256]{5,4,3,1,0,2:T(8,128)(2,1)}, u32[]{:S(2)}, u32[]{:S(2)}) collective-permute-start(bf16[2,2,2,2,128,256]{5,4,3,1,0,2:T(8,128)(2,1)} %copy.84), channel_id=1, source_target_pairs={{0,8},{8,0},{16,24},{24,16},{1,9},{9,1},{17,25},{25,17},{2,10},{10... | collective-permute-start | bytes 3145736 | tf_op jit(solution)/shard_map/ppermute | solution.py:565
  321.8 16.6 %copy-start.6 = (f32[8,4096]{1,0:T(8,128)S(1)}, f32[8,4096]{1,0:T(8,128)}, u32[]{:S(2)}) copy-start(f32[8,4096]{1,0:T(8,128)} %get-tuple-element.31) | copy-start | bytes 393220
  339.3 24.7 %all-to-all-start.2 = ((bf16[32,4,1536]{2,1,0:T(4,128)(2,1)}), bf16[32,4,1536]{2,1,0:T(4,128)(2,1)}, u32[]{:S(2)}, u32[]{:S(2)}) async-start(bf16[32,4,1536]{2,1,0:T(4,128)(2,1)} %bitcast.15), calls=%async_computation.2 | async-start | bytes 786432 | tf_op jit(solution)/shard_map/all_to_all | solution.py:687
  365.2 3.6 copy-start.4
  365.2 3.6 copy-start.5
  367.1 14.0 %collective-permute-start.1 = (bf16[2,2,2,128,256]{4,3,0,1,2:T(8,128)(2,1)S(1)}, bf16[2,2,2,128,256]{4,3,0,1,2:T(8,128)(2,1)S(1)}, u32[]{:S(2)}, u32[]{:S(2)}) collective-permute-start(bf16[2,2,2,128,256]{4,3,0,1,2:T(8,128)(2,1)S(1)} %get-tuple-element.59), channel_id=1, source_target_pairs={{0,16},{8,24},{16,0},{24,8},{1,17},{9,25},{17,1},{25,9},{2,18},{10... | collective-permute-start | bytes 1572872 | tf_op jit(solution)/shard_map/ppermute | solution.py:565
  370.3 14.9 %collective-permute-start.6 = (bf16[2,2,2,128,256]{4,3,1,2,0:T(8,128)(2,1)S(1)}, bf16[2,2,2,128,256]{4,3,1,2,0:T(8,128)(2,1)S(1)}, u32[]{:S(2)}, u32[]{:S(2)}) collective-permute-start(bf16[2,2,2,128,256]{4,3,1,2,0:T(8,128)(2,1)S(1)} %get-tuple-element.61), channel_id=1, source_target_pairs={{0,1},{1,0},{2,3},{3,2},{4,5},{5,4},{6,7},{7,6},{8,9},{9,8},{10,11... | collective-permute-start | bytes 1572872 | tf_op jit(solution)/shard_map/ppermute | solution.py:565
  373.9 40.5 %collective-permute-start.16 = (bf16[2,2,2,256,256]{4,3,1,2,0:T(8,128)(2,1)S(1)}, bf16[2,2,2,256,256]{4,3,1,2,0:T(8,128)(2,1)S(1)}, u32[]{:S(2)}, u32[]{:S(2)}) collective-permute-start(bf16[2,2,2,256,256]{4,3,1,2,0:T(8,128)(2,1)S(1)} %get-tuple-element.45), channel_id=1, source_target_pairs={{0,1},{1,0},{2,3},{3,2},{4,5},{5,4},{6,7},{7,6},{8,9},{9,8},{10,11... | collective-permute-start | bytes 3145736 | tf_op jit(solution)/shard_map/ppermute | solution.py:565
  376.0 13.2 %collective-permute-start.11 = (bf16[2,2,2,128,256]{4,3,2,1,0:T(8,128)(2,1)S(1)}, bf16[2,2,2,128,256]{4,3,2,1,0:T(8,128)(2,1)S(1)}, u32[]{:S(2)}, u32[]{:S(2)}) collective-permute-start(bf16[2,2,2,128,256]{4,3,2,1,0:T(8,128)(2,1)S(1)} %get-tuple-element.49), channel_id=1, source_target_pairs={{0,2},{1,3},{2,0},{3,1},{4,6},{5,7},{6,4},{7,5},{8,10},{9,11},{10,... | collective-permute-start | bytes 1572872 | tf_op jit(solution)/shard_map/ppermute | solution.py:565
  381.2 30.9 %collective-permute-start.2 = (bf16[2,2,128,256]{3,2,0,1:T(8,128)(2,1)S(1)}, bf16[2,2,128,256]{3,2,0,1:T(8,128)(2,1)S(1)}, u32[]{:S(2)}, u32[]{:S(2)}) collective-permute-start(bf16[2,2,128,256]{3,2,0,1:T(8,128)(2,1)S(1)} %get-tuple-element.53), channel_id=1, source_target_pairs={{0,1},{1,0},{2,3},{3,2},{4,5},{5,4},{6,7},{7,6},{8,9},{9,8},{10,11... | collective-permute-start | bytes 786440 | tf_op jit(solution)/shard_map/ppermute | solution.py:565
  385.3 28.4 %collective-permute-start.7 = (bf16[2,2,128,256]{3,2,0,1:T(8,128)(2,1)S(1)}, bf16[2,2,128,256]{3,2,0,1:T(8,128)(2,1)S(1)}, u32[]{:S(2)}, u32[]{:S(2)}) collective-permute-start(bf16[2,2,128,256]{3,2,0,1:T(8,128)(2,1)S(1)} %get-tuple-element.55), channel_id=1, source_target_pairs={{0,16},{8,24},{16,0},{24,8},{1,17},{9,25},{17,1},{25,9},{2,18},{10... | collective-permute-start | bytes 786440 | tf_op jit(solution)/shard_map/ppermute | solution.py:565
  389.3 26.0 %collective-permute-start.12 = (bf16[2,2,128,256]{3,2,1,0:T(8,128)(2,1)S(1)}, bf16[2,2,128,256]{3,2,1,0:T(8,128)(2,1)S(1)}, u32[]{:S(2)}, u32[]{:S(2)}) collective-permute-start(bf16[2,2,128,256]{3,2,1,0:T(8,128)(2,1)S(1)} %get-tuple-element.57), channel_id=1, source_target_pairs={{0,4},{1,5},{2,6},{3,7},{4,0},{5,1},{6,2},{7,3},{8,12},{9,13},{10,... | collective-permute-start | bytes 786440 | tf_op jit(solution)/shard_map/ppermute | solution.py:565
  412.2 5.8 %collective-permute-start.3 = (bf16[2,128,256]{2,1,0:T(8,128)(2,1)S(1)}, bf16[2,128,256]{2,1,0:T(8,128)(2,1)S(1)}, u32[]{:S(2)}, u32[]{:S(2)}) collective-permute-start(bf16[2,128,256]{2,1,0:T(8,128)(2,1)S(1)} %get-tuple-element.65), channel_id=1, source_target_pairs={{0,2},{1,3},{2,0},{3,1},{4,6},{5,7},{6,4},{7,5},{8,10},{9,11},{10,... | collective-permute-start | bytes 393224 | tf_op jit(solution)/shard_map/ppermute | solution.py:565
  413.8 7.2 %collective-permute-start.8 = (bf16[2,128,256]{2,1,0:T(8,128)(2,1)S(1)}, bf16[2,128,256]{2,1,0:T(8,128)(2,1)S(1)}, u32[]{:S(2)}, u32[]{:S(2)}) collective-permute-start(bf16[2,128,256]{2,1,0:T(8,128)(2,1)S(1)} %get-tuple-element.67), channel_id=1, source_target_pairs={{0,2},{1,3},{2,0},{3,1},{4,6},{5,7},{6,4},{7,5},{8,10},{9,11},{10,... | collective-permute-start | bytes 393224 | tf_op jit(solution)/shard_map/ppermute | solution.py:565
  414.8 16.7 %collective-permute-start.17 = (bf16[2,2,256,256]{3,2,0,1:T(8,128)(2,1)S(1)}, bf16[2,2,256,256]{3,2,0,1:T(8,128)(2,1)S(1)}, u32[]{:S(2)}, u32[]{:S(2)}) collective-permute-start(bf16[2,2,256,256]{3,2,0,1:T(8,128)(2,1)S(1)} %get-tuple-element.39), channel_id=1, source_target_pairs={{0,16},{8,24},{16,0},{24,8},{1,17},{9,25},{17,1},{25,9},{2,18},{10... | collective-permute-start | bytes 1572872 | tf_op jit(solution)/shard_map/ppermute | solution.py:565
  415.3 14.6 %collective-permute-start.13 = (bf16[2,128,256]{2,1,0:T(8,128)(2,1)S(1)}, bf16[2,128,256]{2,1,0:T(8,128)(2,1)S(1)}, u32[]{:S(2)}, u32[]{:S(2)}) collective-permute-start(bf16[2,128,256]{2,1,0:T(8,128)(2,1)S(1)} %get-tuple-element.69), channel_id=1, source_target_pairs={{0,16},{8,24},{16,0},{24,8},{1,17},{9,25},{17,1},{25,9},{2,18},{10... | collective-permute-start | bytes 393224 | tf_op jit(solution)/shard_map/ppermute | solution.py:565
  418.0 15.1 %collective-permute-start.4 = (bf16[128,256]{1,0:T(8,128)(2,1)S(1)}, bf16[128,256]{1,0:T(8,128)(2,1)S(1)}, u32[]{:S(2)}, u32[]{:S(2)}) collective-permute-start(bf16[128,256]{1,0:T(8,128)(2,1)S(1)} %fusion.41), channel_id=1, source_target_pairs={{0,4},{1,5},{2,6},{3,7},{4,0},{5,1},{6,2},{7,3},{8,12},{9,13},{10,... | collective-permute-start | bytes 196616 | tf_op jit(solution)/shard_map/ppermute | solution.py:565
  421.0 12.2 %collective-permute-start.9 = (bf16[128,256]{1,0:T(8,128)(2,1)S(1)}, bf16[128,256]{1,0:T(8,128)(2,1)S(1)}, u32[]{:S(2)}, u32[]{:S(2)}) collective-permute-start(bf16[128,256]{1,0:T(8,128)(2,1)S(1)} %fusion.42), channel_id=1, source_target_pairs={{0,4},{1,5},{2,6},{3,7},{4,0},{5,1},{6,2},{7,3},{8,12},{9,13},{10,... | collective-permute-start | bytes 196616 | tf_op jit(solution)/shard_map/ppermute | solution.py:565
  429.9 11.7 %collective-permute-start.14 = (bf16[128,256]{1,0:T(8,128)(2,1)S(1)}, bf16[128,256]{1,0:T(8,128)(2,1)S(1)}, u32[]{:S(2)}, u32[]{:S(2)}) collective-permute-start(bf16[128,256]{1,0:T(8,128)(2,1)S(1)} %fusion.43), channel_id=1, source_target_pairs={{0,1},{1,0},{2,3},{3,2},{4,5},{5,4},{6,7},{7,6},{8,9},{9,8},{10,11... | collective-permute-start | bytes 196616 | tf_op jit(solution)/shard_map/ppermute | solution.py:565
  431.6 6.4 %collective-permute-start.18 = (bf16[2,256,256]{2,1,0:T(8,128)(2,1)S(1)}, bf16[2,256,256]{2,1,0:T(8,128)(2,1)S(1)}, u32[]{:S(2)}, u32[]{:S(2)}) collective-permute-start(bf16[2,256,256]{2,1,0:T(8,128)(2,1)S(1)} %get-tuple-element.51), channel_id=1, source_target_pairs={{0,2},{1,3},{2,0},{3,1},{4,6},{5,7},{6,4},{7,5},{8,10},{9,11},{10,... | collective-permute-start | bytes 786440 | tf_op jit(solution)/shard_map/ppermute | solution.py:565
  433.1 15.9 %copy-start.1 = (bf16[128,1536]{1,0:T(8,128)(2,1)S(1)}, bf16[128,1536]{1,0:T(8,128)(2,1)}, u32[]{:S(2)}) copy-start(bf16[128,1536]{1,0:T(8,128)(2,1)} %param.15) | copy-start | bytes 1179652
  438.0 7.9 %collective-permute-start.19 = (bf16[256,256]{1,0:T(8,128)(2,1)S(1)}, bf16[256,256]{1,0:T(8,128)(2,1)S(1)}, u32[]{:S(2)}, u32[]{:S(2)}) collective-permute-start(bf16[256,256]{1,0:T(8,128)(2,1)S(1)} %fusion.29), channel_id=1, source_target_pairs={{0,4},{1,5},{2,6},{3,7},{4,0},{5,1},{6,2},{7,3},{8,12},{9,13},{10,... | collective-permute-start | bytes 393224 | tf_op jit(solution)/shard_map/ppermute | solution.py:565
  (3 other events, 6.2 us)
Sparse Core Ops, SparseCore 0:
  10.9 77.9 all-gather.2
  92.4 84.6 all-gather.4
  241.5 115.0 reduce-scatter.1
